TPU v7x, 32 devices: a whole 2x2x4 slice. The times are simulated.
32 devices in a mesh: asset: 8 (over z, y), tm: 4 (over x, core).
Axes of the slice: x: 2, y: 2, z: 4, core: 2. Of those that a mesh axis runs over, the one named last changes fastest.
Arguments:
- values: float32 [4, 1024, 16384], P(None, 'tm', 'asset'), may hold values from -64 to 64
- listed_from: int32 [16384], P('asset'), may hold values from -1024 to 1023, as said below
- listed_until: int32 [16384], P('asset'), may hold values from -960 to 3070, as said below
Outputs:
- standardized: float32 [4, 1024, 16384], P(None, 'tm', 'asset')
Inputs may be any that keep to these rules, and one draw needn't show every extreme that they name: listed_until[a] - listed_from[a] is at least 64. listed_until[a] - listed_from[a] is at least 64.
All inputs are finite; a program needn't handle non-finite values.
Results may differ from a plain program's by a relative error of at most 0.00005.
Values sent between devices are 32-bit elements; how exact they have to be, the bound alone decides.
A program may use at most 128 MiB of HBM per device.

v0:
```python
import functools

import jax
import jax.numpy as jnp
from jax import lax
from jax.experimental import pallas as pl
from jax.experimental.pallas import tpu as pltpu
from jax.sharding import PartitionSpec as P

WINDOW = 64
LANES = 128
CLIP = 3.0
UNROLL = 4


def field_groups(fields):
    half = (fields + 1) // 2
    return [(start, min(half, fields - start)) for start in range(0, fields, half)]


def kernel(
    n_tm, n_as, values, opened_hbm, closed_hbm, out,
    x, rolling, weight, inverse, opened_ref, closed_ref, part, got, totals,
    load_sem, halo_send, halo_recv, send_sem, recv_sem,
):
    fields, rows, assets = values.shape
    blocks = rows // WINDOW
    chunks = assets // LANES
    groups = field_groups(fields)
    tm = lax.axis_index("tm")
    me = lax.axis_index("asset")
    later = lax.rem(tm + 1, n_tm)
    before = lax.rem(tm + n_tm - 1, n_tm)

    dates = [
        pltpu.make_async_copy(opened_hbm, opened_ref, load_sem.at[fields]),
        pltpu.make_async_copy(closed_hbm, closed_ref, load_sem.at[fields + 1]),
    ]
    loads = [
        pltpu.make_async_copy(values.at[f], x.at[f, pl.ds(WINDOW, rows)], load_sem.at[f])
        for f in range(fields)
    ]

    barrier = pltpu.get_barrier_semaphore()
    for other in (later, before):
        pl.semaphore_signal(barrier, inc=1, device_id={"tm": other})
    for d in range(1, n_as):
        pl.semaphore_signal(barrier, inc=1, device_id={"asset": lax.rem(me + d, n_as)})
    for copy in dates + loads:
        copy.start()
    pl.semaphore_wait(barrier, n_as + 1)

    halos = [
        pltpu.make_async_remote_copy(
            src_ref=values.at[f, pl.ds(rows - WINDOW, WINDOW)],
            dst_ref=x.at[f, pl.ds(0, WINDOW)],
            send_sem=halo_send.at[f],
            recv_sem=halo_recv.at[f],
            device_id={"tm": later},
        )
        for f in range(fields)
    ]
    for copy in halos:
        copy.start()

    def send(slot):
        for d in range(1, n_as):
            pltpu.make_async_remote_copy(
                src_ref=part.at[slot],
                dst_ref=got.at[slot, d - 1],
                send_sem=send_sem.at[slot],
                recv_sem=recv_sem.at[slot],
                device_id={"asset": lax.rem(me + d, n_as)},
            ).start()

    def receive(slot):
        arrived = got.at[slot]
        pltpu.make_async_copy(arrived, arrived, recv_sem.at[slot]).wait()
        return part[slot] + jnp.sum(got[slot], axis=0)

    def row_of(first, second):
        return jnp.sum(jnp.concatenate([first, second], axis=0).T, axis=0, keepdims=True)

    def factors(row, count):
        mean = row / jnp.maximum(count, 1.0)
        other = pltpu.roll(mean, WINDOW, 1)
        scale = 1.0 / jnp.sqrt(jnp.maximum(mean - other * other, 0.0) + 0.1)
        lane = lax.broadcasted_iota(jnp.int32, row.shape, 1)
        both = jnp.broadcast_to(jnp.where(lane < WINDOW, mean, scale), (LANES, LANES)).T
        return both[:WINDOW], both[WINDOW:]

    def columns(c):
        return pl.ds(pl.multiple_of(c * LANES, LANES), LANES)

    zero = jnp.zeros((WINDOW, LANES), jnp.float32)
    part[...] = jnp.zeros(part.shape, part.dtype)
    first_stamp = tm * rows - WINDOW
    for copy in dates:
        copy.wait()

    @pl.loop(0, blocks + 1)
    def listing(b):
        start = pl.multiple_of(b * WINDOW, WINDOW)
        stamps = first_stamp + start + lax.broadcasted_iota(jnp.int32, (WINDOW, LANES), 0)

        def chunk(c, total):
            cols = columns(c)
            opened = jnp.maximum(opened_ref[:, cols], 0)
            closed = closed_ref[:, cols]
            listed = (stamps >= opened) & (stamps < closed)
            low = jnp.maximum(stamps - (WINDOW - 1), opened)
            counted = jnp.maximum(jnp.minimum(stamps + 1, closed) - low, 1).astype(jnp.float32)
            ones = jnp.where(listed, 1.0, 0.0)
            weight[pl.ds(start, WINDOW), cols] = ones
            inverse[pl.ds(start, WINDOW), cols] = ones / counted
            return total + ones

        total = lax.fori_loop(0, chunks, chunk, zero, unroll=2)
        part[0, pl.ds(lax.rem(b + blocks, blocks + 1), 1), :] = row_of(total, total)

    send(0)

    def roll_window(f, b):
        top = pl.multiple_of(b * WINDOW, WINDOW)

        def chunk(c, carry):
            cols = columns(c)
            reach = pl.ds(top, 2 * WINDOW)
            sums = x[f, reach, cols] * weight[reach, cols]
            for step in (8, 16, 32):
                sums = sums[step:] + sums[:-step]
            for step in (1, 2, 4):
                sums = sums + pltpu.roll(sums, step, 0)
            means = sums[8:] * inverse[pl.ds(top + WINDOW, WINDOW), cols]
            rolling[f, pl.ds(top, WINDOW), cols] = means
            return carry[0] + means, carry[1] + means * means

        return row_of(*lax.fori_loop(0, chunks, chunk, (zero, zero), unroll=UNROLL))

    def clip_scores(f, b, center, scale):
        top = pl.multiple_of(b * WINDOW, WINDOW)

        def chunk(c, carry):
            cols = columns(c)
            scored = (rolling[f, pl.ds(top, WINDOW), cols] - center) * scale
            clipped = jnp.minimum(jnp.maximum(scored, -CLIP), CLIP)
            masked = clipped * weight[pl.ds(top + WINDOW, WINDOW), cols]
            return carry[0] + masked, carry[1] + masked * clipped

        return row_of(*lax.fori_loop(0, chunks, chunk, (zero, zero), unroll=UNROLL))

    def finish(f, b, first, second):
        top = pl.multiple_of(b * WINDOW, WINDOW)
        center, scale = first
        middle, factor = second

        @pl.loop(0, chunks, unroll=UNROLL)
        def chunk(c):
            cols = columns(c)
            here = pl.ds(top, WINDOW)
            scored = (rolling[f, here, cols] - center) * scale
            clipped = jnp.minimum(jnp.maximum(scored, -CLIP), CLIP)
            deviate = (clipped - middle) * weight[pl.ds(top + WINDOW, WINDOW), cols]
            out[f, here, cols] = deviate * factor

    def count_row(b):
        return totals[0, pl.ds(b, 1), :]

    def total_row(slot, i):
        return totals[slot, pl.ds(i, 1), :]

    def main_first(g):
        start, size = groups[g]
        for f in range(start, start + size):
            loads[f].wait()

        @pl.loop(0, size * (blocks - 1))
        def item(i):
            f, b = start + lax.rem(i, size), 1 + lax.div(i, size)
            part[1 + 2 * g, pl.ds(i, 1), :] = roll_window(f, b)

        send(1 + 2 * g)

    def main_second(g):
        start, size = groups[g]
        slot = 1 + 2 * g
        totals[slot] = receive(slot)

        @pl.loop(0, size * (blocks - 1))
        def item(i):
            f, b = start + lax.rem(i, size), 1 + lax.div(i, size)
            center, scale = factors(total_row(slot, i), count_row(b))
            part[slot + 1, pl.ds(i, 1), :] = clip_scores(f, b, center, scale)

        send(slot + 1)

    def main_third(g):
        start, size = groups[g]
        slot = 1 + 2 * g
        totals[slot + 1] = receive(slot + 1)

        @pl.loop(0, size * (blocks - 1))
        def item(i):
            f, b = start + lax.rem(i, size), 1 + lax.div(i, size)
            count = count_row(b)
            first = factors(total_row(slot, i), count)
            finish(f, b, first, factors(total_row(slot + 1, i), count))

    tail_slot = 1 + 2 * len(groups)

    def tail_first(f):
        slot = tail_slot + 2 * f
        halos[f].wait_recv()
        part[slot, :1, :] = roll_window(f, 0)
        send(slot)

    def tail_second(f):
        slot = tail_slot + 2 * f
        totals[slot] = receive(slot)
        center, scale = factors(total_row(slot, 0), count_row(0))
        part[slot + 1, :1, :] = clip_scores(f, 0, center, scale)
        send(slot + 1)

    def tail_third(f):
        slot = tail_slot + 2 * f
        totals[slot + 1] = receive(slot + 1)
        first = factors(total_row(slot, 0), count_row(0))
        finish(f, 0, first, factors(total_row(slot + 1, 0), count_row(0)))

    early = min(2, fields)
    for g in range(len(groups)):
        main_first(g)
    totals[0] = receive(0)
    for step in range(max(early, len(groups))):
        if step < early:
            tail_first(step)
        if step < len(groups):
            main_second(step)
    for step in range(max(early, len(groups))):
        if step < early:
            tail_second(step)
        if step < len(groups):
            main_third(step)
    for f in range(early, fields):
        tail_first(f)
        if f > early:
            tail_second(f - 1)
        tail_third(f - early)
    if fields > early:
        tail_second(fields - 1)
    for f in range(fields - early, fields):
        tail_third(f)

    for copy in halos:
        copy.wait_send()
    for slot in range(part.shape[0]):
        sent = got.at[slot]
        pltpu.make_async_copy(sent, sent, send_sem.at[slot]).wait()


def per_device(n_tm, n_as, values, listed_from, listed_until):
    fields, rows, assets = values.shape
    blocks = rows // WINDOW
    groups = field_groups(fields)
    stats = -(-max(groups[0][1] * (blocks - 1), blocks + 1) // 8) * 8
    slots = 1 + 2 * len(groups) + 2 * fields
    f32 = jnp.float32
    vmem = pltpu.VMEM
    dma = pltpu.SemaphoreType.DMA
    return pl.pallas_call(
        functools.partial(kernel, n_tm, n_as),
        out_shape=vmem((fields, rows, assets), f32),
        in_specs=[pl.BlockSpec(memory_space=pltpu.HBM)] * 3,
        out_specs=pl.BlockSpec(memory_space=vmem),
        scratch_shapes=[
            vmem((fields, WINDOW + rows, assets), f32),
            vmem((fields, rows, assets), f32),
            vmem((WINDOW + rows, assets), f32),
            vmem((WINDOW + rows, assets), f32),
            vmem((1, assets), jnp.int32),
            vmem((1, assets), jnp.int32),
            vmem((slots, stats, LANES), f32),
            vmem((slots, n_as - 1, stats, LANES), f32),
            vmem((slots, stats, LANES), f32),
            dma((fields + 2,)),
            dma((fields,)),
            dma((fields,)),
            dma((slots,)),
            dma((slots,)),
        ],
        compiler_params=pltpu.CompilerParams(
            collective_id=0, has_side_effects=True, vmem_limit_bytes=48 * 2**20
        ),
    )(values, listed_from[None], listed_until[None])


def solution(mesh):
    in_specs = (P(None, "tm", "asset"), P("asset"), P("asset"))
    out_specs = P(None, "tm", "asset")
    body = functools.partial(per_device, mesh.shape["tm"], mesh.shape["asset"])
    return jax.shard_map(
        body, mesh=mesh, in_specs=in_specs, out_specs=out_specs, check_vma=False
    )
```

profile of v0, /device:TPU:0, one launch (start us, length us, event | category | flops | bytes accessed | tf_op | source)
XLA Modules:
  0.0 44.0 jit_solution(13742465517196990218)
XLA Ops:
  0.0 40.6 %shard_map.37 = f32[4,256,2048]{2,1,0:T(8,128)S(1)} custom-call(f32[4,256,2048]{2,1,0:T(8,128)} %values.1, s32[1,2048]{1,0:T(1,128)} %bitcast.2, s32[1,2048]{1,0:T(1,128)} %bitcast.3), custom_call_target="tpu_custom_call" | custom-call | tf_op jit(solution)/shard_map/pallas_call | solution.py:270
  40.6 3.4 %copy.5 = f32[4,256,2048]{2,1,0:T(8,128)} copy(f32[4,256,2048]{2,1,0:T(8,128)S(1)} %shard_map.37) | data formatting | bytes 16777216
where the time goes:
time: 44.1 us; the launch traced here: 44 us
  Pallas kernels  40.6 us (92%)
  local copies, waits for them, and re-layouts  3.4 us (8%)
    pallas_call x1, Pallas kernels, per_device(): pl.pallas_call(functools.partial(kernel, n_tm, n_as), out_shape=vmem((fie...  40.6 us
    unnamed x1, local copies, waits for them, and re-layouts  3.4 us

commit v1 on v0

v1 whole, which is shorter than its diff:
```python
import functools

import jax
import jax.numpy as jnp
from jax import lax
from jax.experimental import pallas as pl
from jax.experimental.pallas import tpu as pltpu
from jax.sharding import PartitionSpec as P

WINDOW = 64
LANES = 128
CLIP = 3.0
UNROLL = 4
PIECES = 4
HELD = 2


def field_groups(fields):
    half = (fields + 1) // 2
    return [(start, min(half, fields - start)) for start in range(0, fields, half)]


def halo_pieces(fields, chunks):
    cuts = PIECES if chunks % PIECES == 0 else 1
    whole = [(f, 0, chunks) for f in range(fields - 1)]
    size = chunks // cuts
    return whole + [(fields - 1, c * size, size) for c in range(cuts)]


def kernel(
    n_tm, n_as, values, opened_hbm, closed_hbm, out,
    x, rolling, weight, inverse, opened_ref, closed_ref, part, got, totals, advice, advised,
    load_sem, halo_send, halo_recv, back_send, back_recv, advice_sem, send_sem, recv_sem,
):
    fields, rows, assets = values.shape
    blocks = rows // WINDOW
    chunks = assets // LANES
    groups = field_groups(fields)
    own = groups[0][1]
    helped = fields - own
    tm = lax.axis_index("tm")
    me = lax.axis_index("asset")
    later = lax.rem(tm + 1, n_tm)
    before = lax.rem(tm + n_tm - 1, n_tm)
    has_next = tm < n_tm - 1
    has_prev = tm > 0

    dates = [
        pltpu.make_async_copy(opened_hbm, opened_ref, load_sem.at[fields]),
        pltpu.make_async_copy(closed_hbm, closed_ref, load_sem.at[fields + 1]),
    ]
    loads = [
        pltpu.make_async_copy(values.at[f], x.at[f, pl.ds(WINDOW, rows)], load_sem.at[f])
        for f in range(fields)
    ]

    barrier = pltpu.get_barrier_semaphore()
    for other in (later, before):
        pl.semaphore_signal(barrier, inc=1, device_id={"tm": other})
    for d in range(1, n_as):
        pl.semaphore_signal(barrier, inc=1, device_id={"asset": lax.rem(me + d, n_as)})
    for copy in dates + loads:
        copy.start()
    pl.semaphore_wait(barrier, n_as + 1)

    pieces = halo_pieces(fields, chunks)
    halos = []
    for i, (f, first, size) in enumerate(pieces):
        cols = pl.ds(first * LANES, size * LANES)
        halos.append(pltpu.make_async_remote_copy(
            src_ref=values.at[f, pl.ds(rows - WINDOW, WINDOW), cols],
            dst_ref=x.at[f, pl.ds(0, WINDOW), cols],
            send_sem=halo_send.at[i],
            recv_sem=halo_recv.at[i],
            device_id={"tm": later},
        ))
    backs = [
        pltpu.make_async_remote_copy(
            src_ref=values.at[f, pl.ds(0, WINDOW)],
            dst_ref=x.at[f, pl.ds(WINDOW + rows, WINDOW)],
            send_sem=back_send.at[f - own],
            recv_sem=back_recv.at[f - own],
            device_id={"tm": before},
        )
        for f in range(own, fields)
    ]
    advising = pltpu.make_async_remote_copy(
        src_ref=advice,
        dst_ref=advised,
        send_sem=advice_sem.at[0],
        recv_sem=advice_sem.at[1],
        device_id={"tm": later},
    )
    free = len(halos) - min(HELD, len(halos) - (fields - 1))

    @pl.when(has_next)
    def _():
        for copy in halos[:free]:
            copy.start()

    @pl.when(has_prev)
    def _():
        for copy in backs:
            copy.start()

    def send(slot):
        for d in range(1, n_as):
            pltpu.make_async_remote_copy(
                src_ref=part.at[slot],
                dst_ref=got.at[slot, d - 1],
                send_sem=send_sem.at[slot],
                recv_sem=recv_sem.at[slot],
                device_id={"asset": lax.rem(me + d, n_as)},
            ).start()

    def receive(slot):
        arrived = got.at[slot]
        pltpu.make_async_copy(arrived, arrived, recv_sem.at[slot]).wait()
        totals[slot] = part[slot] + jnp.sum(got[slot], axis=0)

    def row_of(first, second):
        return jnp.sum(jnp.concatenate([first, second], axis=0).T, axis=0, keepdims=True)

    def factors(row, count):
        mean = row / jnp.maximum(count, 1.0)
        other = pltpu.roll(mean, WINDOW, 1)
        scale = 1.0 / jnp.sqrt(jnp.maximum(mean - other * other, 0.0) + 0.1)
        lane = lax.broadcasted_iota(jnp.int32, row.shape, 1)
        both = jnp.broadcast_to(jnp.where(lane < WINDOW, mean, scale), (LANES, LANES)).T
        return both[:WINDOW], both[WINDOW:]

    def columns(c):
        return pl.ds(pl.multiple_of(c * LANES, LANES), LANES)

    zero = jnp.zeros((WINDOW, LANES), jnp.float32)
    part[...] = jnp.zeros(part.shape, part.dtype)
    first_stamp = tm * rows - WINDOW
    for copy in dates:
        copy.wait()

    @pl.when(tm == 0)
    def _():
        @pl.loop(0, fields)
        def clear(f):
            x[f, pl.ds(0, WINDOW), :] = jnp.zeros((WINDOW, assets), jnp.float32)

    @pl.loop(0, blocks + 2)
    def listing(b):
        start = pl.multiple_of(b * WINDOW, WINDOW)
        stamps = first_stamp + start + lax.broadcasted_iota(jnp.int32, (WINDOW, LANES), 0)

        def chunk(c, total):
            cols = columns(c)
            opened = jnp.maximum(opened_ref[:, cols], 0)
            closed = closed_ref[:, cols]
            listed = (stamps >= opened) & (stamps < closed)
            low = jnp.maximum(stamps - (WINDOW - 1), opened)
            counted = jnp.maximum(jnp.minimum(stamps + 1, closed) - low, 1).astype(jnp.float32)
            ones = jnp.where(listed, 1.0, 0.0)
            weight[pl.ds(start, WINDOW), cols] = ones
            inverse[pl.ds(start, WINDOW), cols] = ones / counted
            return total + ones

        total = lax.fori_loop(0, chunks, chunk, zero, unroll=2)
        part[0, pl.ds(lax.rem(b + blocks + 1, blocks + 2), 1), :] = row_of(total, total)

    send(0)

    def window_means(f, b, c):
        top = pl.multiple_of(b * WINDOW, WINDOW)
        cols = columns(c)
        reach = pl.ds(top, 2 * WINDOW)
        sums = x[f, reach, cols] * weight[reach, cols]
        for step in (8, 16, 32):
            sums = sums[step:] + sums[:-step]
        for step in (1, 2, 4):
            sums = sums + pltpu.roll(sums, step, 0)
        return sums[8:] * inverse[pl.ds(top + WINDOW, WINDOW), cols]

    def roll_window(f, b):
        top = pl.multiple_of(b * WINDOW, WINDOW)

        def chunk(c, carry):
            means = window_means(f, b, c)
            rolling[f, pl.ds(top, WINDOW), columns(c)] = means
            return carry[0] + means, carry[1] + means * means

        return row_of(*lax.fori_loop(0, chunks, chunk, (zero, zero), unroll=UNROLL))

    def clip_scores(f, b, center, scale):
        top = pl.multiple_of(b * WINDOW, WINDOW)

        def chunk(c, carry):
            cols = columns(c)
            scored = (rolling[f, pl.ds(top, WINDOW), cols] - center) * scale
            clipped = jnp.minimum(jnp.maximum(scored, -CLIP), CLIP)
            masked = clipped * weight[pl.ds(top + WINDOW, WINDOW), cols]
            return carry[0] + masked, carry[1] + masked * clipped

        return row_of(*lax.fori_loop(0, chunks, chunk, (zero, zero), unroll=UNROLL))

    def standardized(means, b, cols, first, second):
        center, scale = first
        middle, factor = second
        top = pl.multiple_of(b * WINDOW, WINDOW)
        clipped = jnp.minimum(jnp.maximum((means - center) * scale, -CLIP), CLIP)
        return (clipped - middle) * weight[pl.ds(top + WINDOW, WINDOW), cols] * factor

    def finish(f, b, first, second):
        here = pl.ds(pl.multiple_of(b * WINDOW, WINDOW), WINDOW)

        @pl.loop(0, chunks, unroll=UNROLL)
        def chunk(c):
            cols = columns(c)
            out[f, here, cols] = standardized(rolling[f, here, cols], b, cols, first, second)

    def roll_finish(f, low, size, first, second):
        @pl.loop(low, low + size, unroll=min(UNROLL, size))
        def chunk(c):
            cols = columns(c)
            out[f, :WINDOW, cols] = standardized(window_means(f, 0, c), 0, cols, first, second)

    def count_row(b):
        return totals[0, pl.ds(b, 1), :]

    def total_row(slot, i):
        return totals[slot, pl.ds(i, 1), :]

    def main_items(g):
        size = groups[g][1]
        return pl.loop(jnp.where(tm == 0, 0, size), size * blocks)

    def main_first(g):
        start, size = groups[g]
        for f in range(start, start + size):
            loads[f].wait()

        @main_items(g)
        def item(i):
            f, b = start + lax.rem(i, size), lax.div(i, size)
            part[1 + 2 * g, pl.ds(i, 1), :] = roll_window(f, b)

        send(1 + 2 * g)

    def main_second(g):
        start, size = groups[g]
        slot = 1 + 2 * g
        receive(slot)

        @main_items(g)
        def item(i):
            f, b = start + lax.rem(i, size), lax.div(i, size)
            center, scale = factors(total_row(slot, i), count_row(b))
            part[slot + 1, pl.ds(i, 1), :] = clip_scores(f, b, center, scale)

        send(slot + 1)

    def main_third(g):
        start, size = groups[g]
        slot = 1 + 2 * g
        receive(slot + 1)

        @main_items(g)
        def item(i):
            f, b = start + lax.rem(i, size), lax.div(i, size)
            count = count_row(b)
            first = factors(total_row(slot, i), count)
            finish(f, b, first, factors(total_row(slot + 1, i), count))

    tail_slot = 1 + 2 * len(groups)

    def tail_first(u):
        slot = tail_slot + 2 * u

        @pl.when(has_prev)
        def _():
            halos[u].wait_recv()
            part[slot, :1, :] = roll_window(u, 0)

        if u < helped:
            @pl.when(has_next)
            def _():
                backs[u].wait_recv()
                part[slot, 1:2, :] = roll_window(own + u, blocks)

        send(slot)

    def tail_second(u):
        slot = tail_slot + 2 * u
        receive(slot)

        @pl.when(has_prev)
        def _():
            center, scale = factors(total_row(slot, 0), count_row(0))
            part[slot + 1, :1, :] = clip_scores(u, 0, center, scale)

        if u < helped:
            @pl.when(has_next)
            def _():
                center, scale = factors(total_row(slot, 1), count_row(blocks))
                part[slot + 1, 1:2, :] = clip_scores(own + u, blocks, center, scale)

        send(slot + 1)

    def tail_third(u):
        slot = tail_slot + 2 * u
        receive(slot + 1)
        if u < helped:
            advice[2 * u:2 * u + 1, :] = total_row(slot, 1)
            advice[2 * u + 1:2 * u + 2, :] = total_row(slot + 1, 1)

    def tail_finish(u):
        slot = tail_slot + 2 * u

        @pl.when(has_prev)
        def _():
            first = factors(total_row(slot, 0), count_row(0))
            finish(u, 0, first, factors(total_row(slot + 1, 0), count_row(0)))

    for g in range(len(groups)):
        main_first(g)
    receive(0)
    for g in range(len(groups)):
        main_second(g)
    for g in range(len(groups)):
        main_third(g)
    for u in range(own):
        tail_first(u)
    for u in range(own):
        tail_second(u)
    for u in range(own):
        tail_third(u)

    @pl.when(has_next)
    def _():
        advising.start()
        for copy in halos[free:]:
            copy.start()

    for u in range(own):
        tail_finish(u)

    @pl.when(has_prev)
    def _():
        advising.wait_recv()
        both = {}
        for f in range(own, fields):
            i = 2 * (f - own)
            both[f] = (
                factors(advised[i:i + 1, :], count_row(0)),
                factors(advised[i + 1:i + 2, :], count_row(0)),
            )
        for copy, (f, low, size) in list(zip(halos, pieces))[own:]:
            copy.wait_recv()
            roll_finish(f, low, size, *both[f])
        for copy in backs:
            copy.wait_send()

    @pl.when(has_next)
    def _():
        advising.wait_send()
        for copy in halos:
            copy.wait_send()

    for slot in range(part.shape[0]):
        sent = got.at[slot]
        pltpu.make_async_copy(sent, sent, send_sem.at[slot]).wait()


def per_device(n_tm, n_as, values, listed_from, listed_until):
    fields, rows, assets = values.shape
    blocks = rows // WINDOW
    groups = field_groups(fields)
    own = groups[0][1]
    stats = -(-max(own * blocks, blocks + 2) // 8) * 8
    slots = 1 + 2 * len(groups) + 2 * own
    cuts = len(halo_pieces(fields, assets // LANES))
    f32 = jnp.float32
    vmem = pltpu.VMEM
    dma = pltpu.SemaphoreType.DMA
    return pl.pallas_call(
        functools.partial(kernel, n_tm, n_as),
        out_shape=vmem((fields, rows, assets), f32),
        in_specs=[pl.BlockSpec(memory_space=pltpu.HBM)] * 3,
        out_specs=pl.BlockSpec(memory_space=vmem),
        scratch_shapes=[
            vmem((fields, WINDOW + rows + WINDOW, assets), f32),
            vmem((fields, rows + WINDOW, assets), f32),
            vmem((WINDOW + rows + WINDOW, assets), f32),
            vmem((WINDOW + rows + WINDOW, assets), f32),
            vmem((1, assets), jnp.int32),
            vmem((1, assets), jnp.int32),
            vmem((slots, stats, LANES), f32),
            vmem((slots, n_as - 1, stats, LANES), f32),
            vmem((slots, stats, LANES), f32),
            vmem((max(8, 2 * own), LANES), f32),
            vmem((max(8, 2 * own), LANES), f32),
            dma((fields + 2,)),
            dma((cuts,)),
            dma((cuts,)),
            dma((own,)),
            dma((own,)),
            dma((2,)),
            dma((slots,)),
            dma((slots,)),
        ],
        compiler_params=pltpu.CompilerParams(
            collective_id=0, has_side_effects=True, vmem_limit_bytes=48 * 2**20
        ),
    )(values, listed_from[None], listed_until[None])


def solution(mesh):
    in_specs = (P(None, "tm", "asset"), P("asset"), P("asset"))
    out_specs = P(None, "tm", "asset")
    body = functools.partial(per_device, mesh.shape["tm"], mesh.shape["asset"])
    return jax.shard_map(
        body, mesh=mesh, in_specs=in_specs, out_specs=out_specs, check_vma=False
    )
```

time: 44.1 us -> 50.3 us (1.14)
  the two profiles are of different devices: /device:TPU:0 before, /device:TPU:1 now
where the time goes in v1:
time: 50.3 us; the launch traced here: 50.2 us
  Pallas kernels  46.8 us (93%)
  local copies, waits for them, and re-layouts  3.4 us (7%)
    pallas_call x1, Pallas kernels, per_device(): pl.pallas_call(functools.partial(kernel, n_tm, n_as), out_shape=vmem((fie...  46.8 us
    unnamed x1, local copies, waits for them, and re-layouts  3.4 us

profile of v1, /device:TPU:1, one launch (start us, length us, event | category | flops | bytes accessed | tf_op | source)
XLA Modules:
  0.0 50.2 jit_solution(16268922863347840809)
XLA Ops:
  0.0 46.8 %shard_map.37 = f32[4,256,2048]{2,1,0:T(8,128)S(1)} custom-call(f32[4,256,2048]{2,1,0:T(8,128)} %values.1, s32[1,2048]{1,0:T(1,128)} %bitcast.2, s32[1,2048]{1,0:T(1,128)} %bitcast.3), custom_call_target="tpu_custom_call" | custom-call | tf_op jit(solution)/shard_map/pallas_call | solution.py:381
  46.8 3.4 %copy.5 = f32[4,256,2048]{2,1,0:T(8,128)} copy(f32[4,256,2048]{2,1,0:T(8,128)S(1)} %shard_map.37) | data formatting | bytes 16777216

commit v2 on v1

v2 whole, which is shorter than its diff:
```python
import functools

import jax
import jax.numpy as jnp
from jax import lax
from jax.experimental import pallas as pl
from jax.experimental.pallas import tpu as pltpu
from jax.sharding import PartitionSpec as P

WINDOW = 64
LANES = 128
SUBLANES = 8
CLIP = 3.0
ROLL_UNROLL = 4
UNROLL = 4
PIECES = 8
HELD = 2


def field_groups(fields):
    half = (fields + 1) // 2
    return [(start, min(half, fields - start)) for start in range(0, fields, half)]


def halo_pieces(fields, chunks):
    cuts = PIECES if chunks % PIECES == 0 else 1
    whole = [(f, 0, chunks) for f in range(fields - 1)]
    size = chunks // cuts
    return whole + [(fields - 1, c * size, size) for c in range(cuts)]


def kernel(
    n_tm, n_as, values, opened_hbm, closed_hbm, out,
    x, rolling, weight, inverse, opened_ref, closed_ref,
    acc, columns_of, part, got, totals, counts, advice, advised,
    load_sem, halo_send, halo_recv, back_send, back_recv, advice_sem, send_sem, recv_sem,
):
    fields, rows, assets = values.shape
    blocks = rows // WINDOW
    chunks = assets // LANES
    tiles = WINDOW // SUBLANES
    groups = field_groups(fields)
    own = groups[0][1]
    helped = fields - own
    tm = lax.axis_index("tm")
    me = lax.axis_index("asset")
    later = lax.rem(tm + 1, n_tm)
    before = lax.rem(tm + n_tm - 1, n_tm)
    has_next = tm < n_tm - 1
    has_prev = tm > 0

    dates = [
        pltpu.make_async_copy(opened_hbm, opened_ref, load_sem.at[fields]),
        pltpu.make_async_copy(closed_hbm, closed_ref, load_sem.at[fields + 1]),
    ]
    loads = [
        pltpu.make_async_copy(values.at[f], x.at[f, pl.ds(WINDOW, rows)], load_sem.at[f])
        for f in range(fields)
    ]

    barrier = pltpu.get_barrier_semaphore()
    for other in (later, before):
        pl.semaphore_signal(barrier, inc=1, device_id={"tm": other})
    for d in range(1, n_as):
        pl.semaphore_signal(barrier, inc=1, device_id={"asset": lax.rem(me + d, n_as)})
    for copy in dates + loads:
        copy.start()

    pieces = halo_pieces(fields, chunks)
    halos = []
    for i, (f, first, size) in enumerate(pieces):
        cols = pl.ds(first * LANES, size * LANES)
        halos.append(pltpu.make_async_remote_copy(
            src_ref=values.at[f, pl.ds(rows - WINDOW, WINDOW), cols],
            dst_ref=x.at[f, pl.ds(0, WINDOW), cols],
            send_sem=halo_send.at[i],
            recv_sem=halo_recv.at[i],
            device_id={"tm": later},
        ))
    backs = [
        pltpu.make_async_remote_copy(
            src_ref=values.at[f, pl.ds(0, WINDOW)],
            dst_ref=x.at[f, pl.ds(WINDOW + rows, WINDOW)],
            send_sem=back_send.at[f - own],
            recv_sem=back_recv.at[f - own],
            device_id={"tm": before},
        )
        for f in range(own, fields)
    ]
    advising = pltpu.make_async_remote_copy(
        src_ref=advice,
        dst_ref=advised,
        send_sem=advice_sem.at[0],
        recv_sem=advice_sem.at[1],
        device_id={"tm": later},
    )
    free = len(halos) - min(HELD, len(halos) - (fields - 1))

    def send(slot):
        for d in range(1, n_as):
            pltpu.make_async_remote_copy(
                src_ref=part.at[slot],
                dst_ref=got.at[slot, d - 1],
                send_sem=send_sem.at[slot],
                recv_sem=recv_sem.at[slot],
                device_id={"asset": lax.rem(me + d, n_as)},
            ).start()

    def receive(slot):
        arrived = got.at[slot]
        pltpu.make_async_copy(arrived, arrived, recv_sem.at[slot]).wait()
        totals[slot] = part[slot] + jnp.sum(got[slot], axis=0)

    def columns(c):
        return pl.ds(pl.multiple_of(c * LANES, LANES), LANES)

    def reduce_items(slot, items):
        for i in range(items):
            part[slot, i:i + 1, :] = jnp.sum(acc[i].T, axis=0, keepdims=True)

    def spread_items(sums, count, items):
        mean = sums / count
        other = pltpu.roll(mean, WINDOW, 1)
        scale = 1.0 / jnp.sqrt(jnp.maximum(mean - other * other, 0.0) + 0.1)
        lane = lax.broadcasted_iota(jnp.int32, mean.shape, 1)
        row = jnp.where(lane < WINDOW, mean, scale)
        for i in range(items):
            columns_of[i] = jnp.broadcast_to(row[i:i + 1], (LANES, LANES)).T

    def column_pair(i):
        return columns_of[i, :WINDOW, :], columns_of[i, WINDOW:, :]

    zero = jnp.zeros((WINDOW, LANES), jnp.float32)
    part[...] = jnp.zeros(part.shape, part.dtype)
    acc[...] = jnp.zeros(acc.shape, acc.dtype)
    first_stamp = tm * rows - WINDOW
    for copy in dates:
        copy.wait()

    @pl.when(tm == 0)
    def _():
        @pl.loop(0, fields)
        def clear(f):
            x[f, pl.ds(0, WINDOW), :] = jnp.zeros((WINDOW, assets), jnp.float32)

    @pl.loop(0, blocks + 2)
    def listing(b):
        start = pl.multiple_of(b * WINDOW, WINDOW)
        row = lax.broadcasted_iota(jnp.int32, (WINDOW, LANES), 0)
        passed = (first_stamp + start + 1 + row).astype(jnp.float32)

        def chunk(c, total):
            cols = columns(c)
            opened = jnp.maximum(opened_ref[:, cols], 0).astype(jnp.float32)
            closed = closed_ref[:, cols].astype(jnp.float32)
            age = passed - opened
            listed = (age > 0.0) & (passed <= closed)
            ones = jnp.where(listed, 1.0, 0.0)
            weight[pl.ds(start, WINDOW), cols] = ones
            counted = jnp.minimum(jnp.maximum(age, 1.0), float(WINDOW))
            inverse[pl.ds(start, WINDOW), cols] = ones / counted
            return total + ones

        total = lax.fori_loop(0, chunks, chunk, zero, unroll=2)
        at = lax.rem(b + blocks + 1, blocks + 2)
        acc[at, :WINDOW, :] = total
        acc[at, WINDOW:, :] = total

    reduce_items(0, blocks + 1)
    pl.semaphore_wait(barrier, n_as + 1)

    @pl.when(has_next)
    def _():
        for copy in halos[:free]:
            copy.start()

    @pl.when(has_prev)
    def _():
        for copy in backs:
            copy.start()

    send(0)

    def window_means(f, b, c):
        top = pl.multiple_of(b * WINDOW, WINDOW)
        cols = columns(c)
        sublane = lax.broadcasted_iota(jnp.int32, (SUBLANES, LANES), 0)

        ends = range(2 * tiles)
        reach = pl.ds(top, 2 * WINDOW)
        masked = x[f, reach, cols] * weight[reach, cols]
        sums = {j: masked[SUBLANES * j:SUBLANES * (j + 1)] for j in ends}
        step = 1
        while step < tiles:
            sums = {j: sums[j] + sums[j - step] for j in ends if j - step in sums}
            step *= 2
        shift = 1
        while shift < SUBLANES:
            keep = sublane < SUBLANES - shift
            moved = {tiles - 1: sums[tiles - 1]}
            for j in range(tiles, 2 * tiles):
                moved[j] = jnp.where(keep, sums[j], sums[j - 1])
            sums = {j: sums[j] + pltpu.roll(moved[j], shift, 0) for j in moved}
            shift *= 2
        ending = jnp.concatenate([sums[j] for j in range(tiles, 2 * tiles)], axis=0)
        return ending * inverse[pl.ds(top + WINDOW, WINDOW), cols]

    def roll_window(f, b, i):
        top = pl.multiple_of(b * WINDOW, WINDOW)

        def chunk(c, carry):
            means = window_means(f, b, c)
            rolling[f, pl.ds(top, WINDOW), columns(c)] = means
            return carry[0] + means, carry[1] + means * means

        first, second = lax.fori_loop(0, chunks, chunk, (zero, zero), unroll=ROLL_UNROLL)
        acc[i, :WINDOW, :] = first
        acc[i, WINDOW:, :] = second

    def clip_scores(f, b, i):
        top = pl.multiple_of(b * WINDOW, WINDOW)
        center, scale = column_pair(i)

        def chunk(c, carry):
            cols = columns(c)
            here = pl.ds(top, WINDOW)
            scored = (rolling[f, here, cols] - center) * scale
            clipped = jnp.minimum(jnp.maximum(scored, -CLIP), CLIP)
            rolling[f, here, cols] = clipped
            masked = clipped * weight[pl.ds(top + WINDOW, WINDOW), cols]
            return carry[0] + masked, carry[1] + masked * clipped

        first, second = lax.fori_loop(0, chunks, chunk, (zero, zero), unroll=UNROLL)
        acc[i, :WINDOW, :] = first
        acc[i, WINDOW:, :] = second

    def finish(f, b, i):
        top = pl.multiple_of(b * WINDOW, WINDOW)
        middle, factor = column_pair(i)

        @pl.loop(0, chunks, unroll=UNROLL)
        def chunk(c):
            cols = columns(c)
            here = pl.ds(top, WINDOW)
            deviate = (rolling[f, here, cols] - middle) * weight[pl.ds(top + WINDOW, WINDOW), cols]
            out[f, here, cols] = deviate * factor

    def roll_finish(f, low, size, i):
        center, scale = column_pair(i)
        middle, factor = column_pair(i + 1)

        @pl.loop(low, low + size)
        def chunk(c):
            cols = columns(c)
            means = window_means(f, 0, c)
            clipped = jnp.minimum(jnp.maximum((means - center) * scale, -CLIP), CLIP)
            deviate = (clipped - middle) * weight[WINDOW:2 * WINDOW, cols]
            out[f, :WINDOW, cols] = deviate * factor

    def main_items(g):
        size = groups[g][1]
        return pl.loop(jnp.where(tm == 0, 0, size), size * blocks)

    def main_first(g):
        start, size = groups[g]
        for f in range(start, start + size):
            loads[f].wait()

        @main_items(g)
        def item(i):
            roll_window(start + lax.rem(i, size), lax.div(i, size), i)

        reduce_items(1 + 2 * g, size * blocks)
        send(1 + 2 * g)

    def main_counts(g):
        size = groups[g][1]
        for i in range(size * blocks):
            b = i // size
            counts[g, i:i + 1, :] = jnp.maximum(totals[0, b:b + 1, :], 1.0)

    def main_second(g):
        start, size = groups[g]
        slot = 1 + 2 * g
        receive(slot)
        spread_items(totals[slot], counts[g], size * blocks)

        @main_items(g)
        def item(i):
            clip_scores(start + lax.rem(i, size), lax.div(i, size), i)

        reduce_items(slot + 1, size * blocks)
        send(slot + 1)

    def main_third(g):
        start, size = groups[g]
        slot = 2 + 2 * g
        receive(slot)
        spread_items(totals[slot], counts[g], size * blocks)

        @main_items(g)
        def item(i):
            finish(start + lax.rem(i, size), lax.div(i, size), i)

    tail = 1 + 2 * len(groups)
    last = len(groups)

    def tail_first(u):
        @pl.when(has_prev)
        def _():
            halos[u].wait_recv()
            roll_window(u, 0, 2 * u)

        if u < helped:
            @pl.when(has_next)
            def _():
                backs[u].wait_recv()
                roll_window(own + u, blocks, 2 * u + 1)

    def tail_second(u):
        @pl.when(has_prev)
        def _():
            clip_scores(u, 0, 2 * u)

        if u < helped:
            @pl.when(has_next)
            def _():
                clip_scores(own + u, blocks, 2 * u + 1)

    for g in range(len(groups)):
        main_first(g)
    receive(0)
    for i in range(2 * own):
        b = 0 if i % 2 == 0 else blocks
        counts[last, i:i + 1, :] = jnp.maximum(totals[0, b:b + 1, :], 1.0)
    for g in range(len(groups)):
        main_counts(g)
        main_second(g)
    for g in range(len(groups)):
        main_third(g)

    for u in range(own):
        tail_first(u)
    reduce_items(tail, 2 * own)
    send(tail)
    receive(tail)
    spread_items(totals[tail], counts[last], 2 * own)
    for u in range(own):
        tail_second(u)
    reduce_items(tail + 1, 2 * own)
    send(tail + 1)
    receive(tail + 1)
    for u in range(helped):
        i = 2 * u
        advice[i:i + 1, :] = totals[tail, i + 1:i + 2, :]
        advice[i + 1:i + 2, :] = totals[tail + 1, i + 1:i + 2, :]

    @pl.when(has_next)
    def _():
        advising.start()
        for copy in halos[free:]:
            copy.start()

    @pl.when(has_prev)
    def _():
        spread_items(totals[tail + 1], counts[last], 2 * own)
        for u in range(own):
            finish(u, 0, 2 * u)
        advising.wait_recv()
        spread_items(advised[...], jnp.broadcast_to(counts[last, :1, :], advised.shape), 2 * helped)
        for copy, (f, low, size) in list(zip(halos, pieces))[own:]:
            copy.wait_recv()
            roll_finish(f, low, size, 2 * (f - own))
        for copy in backs:
            copy.wait_send()

    @pl.when(has_next)
    def _():
        advising.wait_send()
        for copy in halos:
            copy.wait_send()

    for slot in range(part.shape[0]):
        sent = got.at[slot]
        pltpu.make_async_copy(sent, sent, send_sem.at[slot]).wait()


def per_device(n_tm, n_as, values, listed_from, listed_until):
    fields, rows, assets = values.shape
    blocks = rows // WINDOW
    groups = field_groups(fields)
    own = groups[0][1]
    stats = -(-max(own * blocks, blocks + 2, 2 * own) // SUBLANES) * SUBLANES
    slots = 1 + 2 * len(groups) + 2
    cuts = len(halo_pieces(fields, assets // LANES))
    f32 = jnp.float32
    vmem = pltpu.VMEM
    dma = pltpu.SemaphoreType.DMA
    return pl.pallas_call(
        functools.partial(kernel, n_tm, n_as),
        out_shape=vmem((fields, rows, assets), f32),
        in_specs=[pl.BlockSpec(memory_space=pltpu.HBM)] * 3,
        out_specs=pl.BlockSpec(memory_space=vmem),
        scratch_shapes=[
            vmem((fields, WINDOW + rows + WINDOW, assets), f32),
            vmem((fields, rows + WINDOW, assets), f32),
            vmem((WINDOW + rows + WINDOW, assets), f32),
            vmem((WINDOW + rows + WINDOW, assets), f32),
            vmem((1, assets), jnp.int32),
            vmem((1, assets), jnp.int32),
            vmem((stats, LANES, LANES), f32),
            vmem((stats, LANES, LANES), f32),
            vmem((slots, stats, LANES), f32),
            vmem((slots, n_as - 1, stats, LANES), f32),
            vmem((slots, stats, LANES), f32),
            vmem((len(groups) + 1, stats, LANES), f32),
            vmem((stats, LANES), f32),
            vmem((stats, LANES), f32),
            dma((fields + 2,)),
            dma((cuts,)),
            dma((cuts,)),
            dma((own,)),
            dma((own,)),
            dma((2,)),
            dma((slots,)),
            dma((slots,)),
        ],
        compiler_params=pltpu.CompilerParams(
            collective_id=0, has_side_effects=True, vmem_limit_bytes=48 * 2**20
        ),
    )(values, listed_from[None], listed_until[None])


def solution(mesh):
    in_specs = (P(None, "tm", "asset"), P("asset"), P("asset"))
    out_specs = P(None, "tm", "asset")
    body = functools.partial(per_device, mesh.shape["tm"], mesh.shape["asset"])
    return jax.shard_map(
        body, mesh=mesh, in_specs=in_specs, out_specs=out_specs, check_vma=False
    )
```

time: 50.3 us -> 43.2 us (0.86)
  Pallas kernels: 46.8 us -> 39.6 us
    pallas_call x1, Pallas kernels: 46.8 us -> 39.6 us  [per_device(): pl.pallas_call(functools.partial(kernel, n_tm, n_as), out_shape=vmem((fie...]
where the time goes in v2:
time: 43.2 us; the launch traced here: 43 us
  Pallas kernels  39.6 us (92%)
  local copies, waits for them, and re-layouts  3.4 us (8%)
    pallas_call x1, Pallas kernels, per_device(): pl.pallas_call(functools.partial(kernel, n_tm, n_as), out_shape=vmem((fie...  39.6 us
    unnamed x1, local copies, waits for them, and re-layouts  3.4 us

profile of v2, /device:TPU:1, one launch (start us, length us, event | category | flops | bytes accessed | tf_op | source)
XLA Modules:
  0.0 43.0 jit_solution(7200167864209455237)
XLA Ops:
  0.0 39.6 %shard_map.37 = f32[4,256,2048]{2,1,0:T(8,128)S(1)} custom-call(f32[4,256,2048]{2,1,0:T(8,128)} %values.1, s32[1,2048]{1,0:T(1,128)} %bitcast.2, s32[1,2048]{1,0:T(1,128)} %bitcast.3), custom_call_target="tpu_custom_call" | custom-call | tf_op jit(solution)/shard_map/pallas_call | solution.py:399
  39.6 3.4 %copy.5 = f32[4,256,2048]{2,1,0:T(8,128)} copy(f32[4,256,2048]{2,1,0:T(8,128)S(1)} %shard_map.37) | data formatting | bytes 16777216

commit v3 on v2

--- a/solution.py
+++ b/solution.py
@@ -29,11 +29,17 @@
     return whole + [(fields - 1, c * size, size) for c in range(cuts)]
 
 
+def greeting_rounds(n):
+    if n % 2:
+        return 0
+    return max(n // 2 - 1, 0)
+
+
 def kernel(
     n_tm, n_as, values, opened_hbm, closed_hbm, out,
     x, rolling, weight, inverse, opened_ref, closed_ref,
     acc, columns_of, part, got, totals, counts, advice, advised,
-    load_sem, halo_send, halo_recv, back_send, back_recv, advice_sem, send_sem, recv_sem,
+    load_sem, halo_send, halo_recv, back_send, back_recv, advice_sem, send_sem, recv_sem, hello,
 ):
     fields, rows, assets = values.shape
     blocks = rows // WINDOW
@@ -59,10 +65,36 @@
     ]
 
     barrier = pltpu.get_barrier_semaphore()
-    for other in (later, before):
-        pl.semaphore_signal(barrier, inc=1, device_id={"tm": other})
-    for d in range(1, n_as):
-        pl.semaphore_signal(barrier, inc=1, device_id={"asset": lax.rem(me + d, n_as)})
+    rounds = greeting_rounds(n_as)
+
+    @pl.when(has_next)
+    def _():
+        pl.semaphore_signal(barrier, inc=1, device_id={"tm": later})
+
+    @pl.when(has_prev)
+    def _():
+        pl.semaphore_signal(barrier, inc=1, device_id={"tm": before})
+
+    def greet(semaphore):
+        if n_as % 2:
+            for d in range(1, n_as):
+                pl.semaphore_signal(semaphore, inc=1, device_id={"asset": lax.rem(me + d, n_as)})
+            return n_as - 1
+        beside = me + 1 - 2 * lax.rem(me, 2)
+        pl.semaphore_signal(semaphore, inc=1, device_id={"asset": beside})
+
+        @pl.when(me >= 2)
+        def _():
+            pl.semaphore_signal(semaphore, inc=1, device_id={"asset": me - 2})
+
+        @pl.when(me + 2 < n_as)
+        def _():
+            pl.semaphore_signal(semaphore, inc=1, device_id={"asset": me + 2})
+
+        return 1 + jnp.where(me >= 2, 1, 0) + jnp.where(me + 2 < n_as, 1, 0)
+
+    near = greet(barrier)
+    expected = near + jnp.where(has_next, 1, 0) + jnp.where(has_prev, 1, 0)
     for copy in dates + loads:
         copy.start()
 
@@ -143,7 +175,6 @@
         def clear(f):
             x[f, pl.ds(0, WINDOW), :] = jnp.zeros((WINDOW, assets), jnp.float32)
 
-    @pl.loop(0, blocks + 2)
     def listing(b):
         start = pl.multiple_of(b * WINDOW, WINDOW)
         row = lax.broadcasted_iota(jnp.int32, (WINDOW, LANES), 0)
@@ -166,8 +197,12 @@
         acc[at, :WINDOW, :] = total
         acc[at, WINDOW:, :] = total
 
-    reduce_items(0, blocks + 1)
-    pl.semaphore_wait(barrier, n_as + 1)
+    def listing_blocks(low, high):
+        pl.loop(low, high)(listing)
+
+    ahead = min(2, blocks)
+    listing_blocks(0, ahead)
+    pl.semaphore_wait(barrier, expected)
 
     @pl.when(has_next)
     def _():
@@ -179,7 +214,19 @@
         for copy in backs:
             copy.start()
 
-    send(0)
+    for r in range(rounds):
+        greet(hello.at[r])
+        if r == 0:
+            listing_blocks(ahead, blocks)
+        if r == 1:
+            listing_blocks(blocks, blocks + 2)
+        if r < rounds - 1:
+            pl.semaphore_wait(hello.at[r], near)
+    if rounds < 1:
+        listing_blocks(ahead, blocks)
+    if rounds < 2:
+        listing_blocks(blocks, blocks + 2)
+    reduce_items(0, blocks + 1)
 
     def window_means(f, b, c):
         top = pl.multiple_of(b * WINDOW, WINDOW)
@@ -271,6 +318,10 @@
             roll_window(start + lax.rem(i, size), lax.div(i, size), i)
 
         reduce_items(1 + 2 * g, size * blocks)
+        if g == 0:
+            if rounds:
+                pl.semaphore_wait(hello.at[rounds - 1], near)
+            send(0)
         send(1 + 2 * g)
 
     def main_counts(g):
@@ -326,6 +377,18 @@
             @pl.when(has_next)
             def _():
                 clip_scores(own + u, blocks, 2 * u + 1)
+
+    def tail_exchange():
+        reduce_items(tail, 2 * own)
+        send(tail)
+
+    def tail_scores():
+        receive(tail)
+        spread_items(totals[tail], counts[last], 2 * own)
+        for u in range(own):
+            tail_second(u)
+        reduce_items(tail + 1, 2 * own)
+        send(tail + 1)
 
     for g in range(len(groups)):
         main_first(g)
@@ -336,19 +399,13 @@
     for g in range(len(groups)):
         main_counts(g)
         main_second(g)
-    for g in range(len(groups)):
-        main_third(g)
-
     for u in range(own):
         tail_first(u)
-    reduce_items(tail, 2 * own)
-    send(tail)
-    receive(tail)
-    spread_items(totals[tail], counts[last], 2 * own)
-    for u in range(own):
-        tail_second(u)
-    reduce_items(tail + 1, 2 * own)
-    send(tail + 1)
+    tail_exchange()
+    for g in range(len(groups) - 1):
+        main_third(g)
+    tail_scores()
+    main_third(len(groups) - 1)
     receive(tail + 1)
     for u in range(helped):
         i = 2 * u
@@ -424,6 +481,7 @@
             dma((2,)),
             dma((slots,)),
             dma((slots,)),
+            pltpu.SemaphoreType.REGULAR((max(greeting_rounds(n_as), 1),)),
         ],
         compiler_params=pltpu.CompilerParams(
             collective_id=0, has_side_effects=True, vmem_limit_bytes=48 * 2**20

time: 43.2 us -> 38.4 us (0.89)
  Pallas kernels: 39.6 us -> 34.8 us
    pallas_call x1, Pallas kernels: 39.6 us -> 34.8 us  [per_device(): pl.pallas_call(functools.partial(kernel, n_tm, n_as), out_shape=vmem((fie...]
where the time goes in v3:
time: 38.4 us; the launch traced here: 38.2 us
  Pallas kernels  34.8 us (91%)
  local copies, waits for them, and re-layouts  3.4 us (9%)
    pallas_call x1, Pallas kernels, per_device(): pl.pallas_call(functools.partial(kernel, n_tm, n_as), out_shape=vmem((fie...  34.8 us
    unnamed x1, local copies, waits for them, and re-layouts  3.4 us

profile of v3, /device:TPU:1, one launch (start us, length us, event | category | flops | bytes accessed | tf_op | source)
XLA Modules:
  0.0 38.2 jit_solution(9747304123200715020)
XLA Ops:
  0.0 34.8 %shard_map.37 = f32[4,256,2048]{2,1,0:T(8,128)S(1)} custom-call(f32[4,256,2048]{2,1,0:T(8,128)} %values.1, s32[1,2048]{1,0:T(1,128)} %bitcast.2, s32[1,2048]{1,0:T(1,128)} %bitcast.3), custom_call_target="tpu_custom_call" | custom-call | tf_op jit(solution)/shard_map/pallas_call | solution.py:456
  34.8 3.4 %copy.5 = f32[4,256,2048]{2,1,0:T(8,128)} copy(f32[4,256,2048]{2,1,0:T(8,128)S(1)} %shard_map.37) | data formatting | bytes 16777216

commit v4 on v3

--- a/solution.py
+++ b/solution.py
@@ -48,6 +48,7 @@
     groups = field_groups(fields)
     own = groups[0][1]
     helped = fields - own
+    stats = part.shape[1]
     tm = lax.axis_index("tm")
     me = lax.axis_index("asset")
     later = lax.rem(tm + 1, n_tm)
@@ -60,7 +61,9 @@
         pltpu.make_async_copy(closed_hbm, closed_ref, load_sem.at[fields + 1]),
     ]
     loads = [
-        pltpu.make_async_copy(values.at[f], x.at[f, pl.ds(WINDOW, rows)], load_sem.at[f])
+        pltpu.make_async_copy(
+            values.at[f], x.at[f, pl.ds(WINDOW, rows), pl.ds(0, assets)], load_sem.at[f]
+        )
         for f in range(fields)
     ]
 
@@ -112,7 +115,7 @@
     backs = [
         pltpu.make_async_remote_copy(
             src_ref=values.at[f, pl.ds(0, WINDOW)],
-            dst_ref=x.at[f, pl.ds(WINDOW + rows, WINDOW)],
+            dst_ref=x.at[f, pl.ds(WINDOW + rows, WINDOW), pl.ds(0, assets)],
             send_sem=back_send.at[f - own],
             recv_sem=back_recv.at[f - own],
             device_id={"tm": before},
@@ -146,18 +149,18 @@
     def columns(c):
         return pl.ds(pl.multiple_of(c * LANES, LANES), LANES)
 
-    def reduce_items(slot, items):
+    def reduce_items(slot, items, first=0):
         for i in range(items):
-            part[slot, i:i + 1, :] = jnp.sum(acc[i].T, axis=0, keepdims=True)
-
-    def spread_items(sums, count, items):
+            part[slot, i:i + 1, :] = jnp.sum(acc[first + i].T, axis=0, keepdims=True)
+
+    def spread_items(sums, count, items, first=0):
         mean = sums / count
         other = pltpu.roll(mean, WINDOW, 1)
         scale = 1.0 / jnp.sqrt(jnp.maximum(mean - other * other, 0.0) + 0.1)
         lane = lax.broadcasted_iota(jnp.int32, mean.shape, 1)
         row = jnp.where(lane < WINDOW, mean, scale)
         for i in range(items):
-            columns_of[i] = jnp.broadcast_to(row[i:i + 1], (LANES, LANES)).T
+            columns_of[first + i] = jnp.broadcast_to(row[i:i + 1], (LANES, LANES)).T
 
     def column_pair(i):
         return columns_of[i, :WINDOW, :], columns_of[i, WINDOW:, :]
@@ -173,7 +176,7 @@
     def _():
         @pl.loop(0, fields)
         def clear(f):
-            x[f, pl.ds(0, WINDOW), :] = jnp.zeros((WINDOW, assets), jnp.float32)
+            x[f, pl.ds(0, WINDOW), pl.ds(0, assets)] = jnp.zeros((WINDOW, assets), jnp.float32)
 
     def listing(b):
         start = pl.multiple_of(b * WINDOW, WINDOW)
@@ -292,17 +295,32 @@
             deviate = (rolling[f, here, cols] - middle) * weight[pl.ds(top + WINDOW, WINDOW), cols]
             out[f, here, cols] = deviate * factor
 
-    def roll_finish(f, low, size, i):
-        center, scale = column_pair(i)
-        middle, factor = column_pair(i + 1)
-
-        @pl.loop(low, low + size)
+    def standardized(means, cols, first, second):
+        center, scale = first
+        middle, factor = second
+        clipped = jnp.minimum(jnp.maximum((means - center) * scale, -CLIP), CLIP)
+        return (clipped - middle) * weight[WINDOW:2 * WINDOW, cols] * factor
+
+    def roll_only(f, low, size):
+        @pl.loop(low, low + size, unroll=min(2, size))
+        def chunk(c):
+            rolling[f, :WINDOW, columns(c)] = window_means(f, 0, c)
+
+    def score_finish(f, low, size, i):
+        first, second = column_pair(i), column_pair(i + 1)
+
+        @pl.loop(low, low + size, unroll=min(2, size))
         def chunk(c):
             cols = columns(c)
-            means = window_means(f, 0, c)
-            clipped = jnp.minimum(jnp.maximum((means - center) * scale, -CLIP), CLIP)
-            deviate = (clipped - middle) * weight[WINDOW:2 * WINDOW, cols]
-            out[f, :WINDOW, cols] = deviate * factor
+            out[f, :WINDOW, cols] = standardized(rolling[f, :WINDOW, cols], cols, first, second)
+
+    def roll_finish(f, low, size, i):
+        first, second = column_pair(i), column_pair(i + 1)
+
+        @pl.loop(low, low + size, unroll=min(2, size))
+        def chunk(c):
+            cols = columns(c)
+            out[f, :WINDOW, cols] = standardized(window_means(f, 0, c), cols, first, second)
 
     def main_items(g):
         size = groups[g][1]
@@ -360,38 +378,46 @@
         @pl.when(has_prev)
         def _():
             halos[u].wait_recv()
-            roll_window(u, 0, 2 * u)
+            roll_window(u, 0, stats + 2 * u)
 
         if u < helped:
             @pl.when(has_next)
             def _():
                 backs[u].wait_recv()
-                roll_window(own + u, blocks, 2 * u + 1)
+                roll_window(own + u, blocks, stats + 2 * u + 1)
 
     def tail_second(u):
         @pl.when(has_prev)
         def _():
-            clip_scores(u, 0, 2 * u)
+            clip_scores(u, 0, stats + 2 * u)
 
         if u < helped:
             @pl.when(has_next)
             def _():
-                clip_scores(own + u, blocks, 2 * u + 1)
+                clip_scores(own + u, blocks, stats + 2 * u + 1)
 
     def tail_exchange():
-        reduce_items(tail, 2 * own)
+        reduce_items(tail, 2 * own, stats)
         send(tail)
 
     def tail_scores():
         receive(tail)
-        spread_items(totals[tail], counts[last], 2 * own)
+        spread_items(totals[tail], counts[last], 2 * own, stats)
         for u in range(own):
             tail_second(u)
-        reduce_items(tail + 1, 2 * own)
+        reduce_items(tail + 1, 2 * own, stats)
         send(tail + 1)
 
     for g in range(len(groups)):
         main_first(g)
+    tail_first(0)
+
+    @pl.when(tm == 0)
+    def _():
+        for u in range(1, own):
+            tail_first(u)
+        tail_exchange()
+
     receive(0)
     for i in range(2 * own):
         b = 0 if i % 2 == 0 else blocks
@@ -399,12 +425,24 @@
     for g in range(len(groups)):
         main_counts(g)
         main_second(g)
-    for u in range(own):
-        tail_first(u)
-    tail_exchange()
+
+    @pl.when(tm == 0)
+    def _():
+        tail_scores()
+
+    @pl.when(has_prev)
+    def _():
+        for u in range(1, own):
+            tail_first(u)
+        tail_exchange()
+
     for g in range(len(groups) - 1):
         main_third(g)
-    tail_scores()
+
+    @pl.when(has_prev)
+    def _():
+        tail_scores()
+
     main_third(len(groups) - 1)
     receive(tail + 1)
     for u in range(helped):
@@ -423,9 +461,16 @@
         spread_items(totals[tail + 1], counts[last], 2 * own)
         for u in range(own):
             finish(u, 0, 2 * u)
+        landing = list(zip(halos, pieces))[own:]
+        early = landing[:len(landing) - (len(halos) - free)]
+        for copy, (f, low, size) in early:
+            copy.wait_recv()
+            roll_only(f, low, size)
         advising.wait_recv()
         spread_items(advised[...], jnp.broadcast_to(counts[last, :1, :], advised.shape), 2 * helped)
-        for copy, (f, low, size) in list(zip(halos, pieces))[own:]:
+        for copy, (f, low, size) in early:
+            score_finish(f, low, size, 2 * (f - own))
+        for copy, (f, low, size) in landing[len(early):]:
             copy.wait_recv()
             roll_finish(f, low, size, 2 * (f - own))
         for copy in backs:
@@ -459,14 +504,14 @@
         in_specs=[pl.BlockSpec(memory_space=pltpu.HBM)] * 3,
         out_specs=pl.BlockSpec(memory_space=vmem),
         scratch_shapes=[
-            vmem((fields, WINDOW + rows + WINDOW, assets), f32),
-            vmem((fields, rows + WINDOW, assets), f32),
-            vmem((WINDOW + rows + WINDOW, assets), f32),
-            vmem((WINDOW + rows + WINDOW, assets), f32),
+            vmem((fields, WINDOW + rows + WINDOW, assets + LANES), f32),
+            vmem((fields, rows + WINDOW, assets + LANES), f32),
+            vmem((WINDOW + rows + WINDOW, assets + LANES), f32),
+            vmem((WINDOW + rows + WINDOW, assets + LANES), f32),
             vmem((1, assets), jnp.int32),
             vmem((1, assets), jnp.int32),
-            vmem((stats, LANES, LANES), f32),
-            vmem((stats, LANES, LANES), f32),
+            vmem((stats + 2 * own, LANES, LANES), f32),
+            vmem((stats + 2 * own, LANES, LANES), f32),
             vmem((slots, stats, LANES), f32),
             vmem((slots, n_as - 1, stats, LANES), f32),
             vmem((slots, stats, LANES), f32),

time: 38.4 us -> 32.9 us (0.86)
  the two profiles are of different devices: /device:TPU:1 before, /device:TPU:3 now
where the time goes in v4:
time: 32.9 us; the launch traced here: 32.7 us
  Pallas kernels  29.3 us (89%)
  local copies, waits for them, and re-layouts  3.4 us (10%)
    pallas_call x1, Pallas kernels, per_device(): pl.pallas_call(functools.partial(kernel, n_tm, n_as), out_shape=vmem((fie...  29.3 us
    unnamed x1, local copies, waits for them, and re-layouts  3.4 us

profile of v4, /device:TPU:3, one launch (start us, length us, event | category | flops | bytes accessed | tf_op | source)
XLA Modules:
  0.0 32.7 jit_solution(12125253880753971327)
XLA Ops:
  0.0 29.3 %shard_map.37 = f32[4,256,2048]{2,1,0:T(8,128)S(1)} custom-call(f32[4,256,2048]{2,1,0:T(8,128)} %values.1, s32[1,2048]{1,0:T(1,128)} %bitcast.2, s32[1,2048]{1,0:T(1,128)} %bitcast.3), custom_call_target="tpu_custom_call" | custom-call | tf_op jit(solution)/shard_map/pallas_call | solution.py:501
  29.3 3.4 %copy.5 = f32[4,256,2048]{2,1,0:T(8,128)} copy(f32[4,256,2048]{2,1,0:T(8,128)S(1)} %shard_map.37) | data formatting | bytes 16777216

commit v5 on v4

--- a/solution.py
+++ b/solution.py
@@ -13,8 +13,7 @@
 CLIP = 3.0
 ROLL_UNROLL = 4
 UNROLL = 4
-PIECES = 8
-HELD = 2
+HELD = 1
 
 
 def field_groups(fields):
@@ -23,10 +22,13 @@
 
 
 def halo_pieces(fields, chunks):
-    cuts = PIECES if chunks % PIECES == 0 else 1
-    whole = [(f, 0, chunks) for f in range(fields - 1)]
-    size = chunks // cuts
-    return whole + [(fields - 1, c * size, size) for c in range(cuts)]
+    pieces = [(f, 0, chunks) for f in range(fields - 1)]
+    first, left = 0, chunks
+    while left > 0:
+        size = max(left // 2, 1)
+        pieces.append((fields - 1, first, size))
+        first, left = first + size, left - size
+    return pieces
 
 
 def greeting_rounds(n):
@@ -49,6 +51,8 @@
     own = groups[0][1]
     helped = fields - own
     stats = part.shape[1]
+    tail = 1 + 2 * len(groups)
+    last = len(groups)
     tm = lax.axis_index("tm")
     me = lax.axis_index("asset")
     later = lax.rem(tm + 1, n_tm)
@@ -131,18 +135,21 @@
     )
     free = len(halos) - min(HELD, len(halos) - (fields - 1))
 
+    def rows_of(slot):
+        return pl.ds(0, 2 * own if slot >= tail else stats)
+
     def send(slot):
         for d in range(1, n_as):
             pltpu.make_async_remote_copy(
-                src_ref=part.at[slot],
-                dst_ref=got.at[slot, d - 1],
+                src_ref=part.at[slot, rows_of(slot)],
+                dst_ref=got.at[slot, d - 1, rows_of(slot)],
                 send_sem=send_sem.at[slot],
                 recv_sem=recv_sem.at[slot],
                 device_id={"asset": lax.rem(me + d, n_as)},
             ).start()
 
     def receive(slot):
-        arrived = got.at[slot]
+        arrived = got.at[slot, :, rows_of(slot)]
         pltpu.make_async_copy(arrived, arrived, recv_sem.at[slot]).wait()
         totals[slot] = part[slot] + jnp.sum(got[slot], axis=0)
 
@@ -207,15 +214,15 @@
     listing_blocks(0, ahead)
     pl.semaphore_wait(barrier, expected)
 
-    @pl.when(has_next)
-    def _():
-        for copy in halos[:free]:
-            copy.start()
-
-    @pl.when(has_prev)
-    def _():
-        for copy in backs:
-            copy.start()
+    for i in range(free):
+        @pl.when(has_next)
+        def _():
+            halos[i].start()
+
+        if i < helped:
+            @pl.when(has_prev)
+            def _():
+                backs[i].start()
 
     for r in range(rounds):
         greet(hello.at[r])
@@ -371,9 +378,6 @@
         def item(i):
             finish(start + lax.rem(i, size), lax.div(i, size), i)
 
-    tail = 1 + 2 * len(groups)
-    last = len(groups)
-
     def tail_first(u):
         @pl.when(has_prev)
         def _():
@@ -422,13 +426,8 @@
     for i in range(2 * own):
         b = 0 if i % 2 == 0 else blocks
         counts[last, i:i + 1, :] = jnp.maximum(totals[0, b:b + 1, :], 1.0)
-    for g in range(len(groups)):
-        main_counts(g)
-        main_second(g)
-
-    @pl.when(tm == 0)
-    def _():
-        tail_scores()
+    main_counts(0)
+    main_second(0)
 
     @pl.when(has_prev)
     def _():
@@ -436,6 +435,14 @@
             tail_first(u)
         tail_exchange()
 
+    for g in range(1, len(groups)):
+        main_counts(g)
+        main_second(g)
+
+    @pl.when(tm == 0)
+    def _():
+        tail_scores()
+
     for g in range(len(groups) - 1):
         main_third(g)
 
@@ -444,6 +451,16 @@
         tail_scores()
 
     main_third(len(groups) - 1)
+    landing = list(zip(halos, pieces))[own:]
+    early = landing[:len(landing) - (len(halos) - free)]
+    sooner = [entry for entry in early if entry[1][0] < fields - 1]
+
+    @pl.when(has_prev)
+    def _():
+        for copy, (f, low, size) in sooner:
+            copy.wait_recv()
+            roll_only(f, low, size)
+
     receive(tail + 1)
     for u in range(helped):
         i = 2 * u
@@ -461,9 +478,7 @@
         spread_items(totals[tail + 1], counts[last], 2 * own)
         for u in range(own):
             finish(u, 0, 2 * u)
-        landing = list(zip(halos, pieces))[own:]
-        early = landing[:len(landing) - (len(halos) - free)]
-        for copy, (f, low, size) in early:
+        for copy, (f, low, size) in early[len(sooner):]:
             copy.wait_recv()
             roll_only(f, low, size)
         advising.wait_recv()
@@ -483,7 +498,7 @@
             copy.wait_send()
 
     for slot in range(part.shape[0]):
-        sent = got.at[slot]
+        sent = got.at[slot, :, rows_of(slot)]
         pltpu.make_async_copy(sent, sent, send_sem.at[slot]).wait()
 
 

time: 32.9 us -> 31.2 us (0.948)
  the two profiles are of different devices: /device:TPU:3 before, /device:TPU:1 now
where the time goes in v5:
time: 31.2 us; the launch traced here: 31 us
  Pallas kernels  27.6 us (88%)
  local copies, waits for them, and re-layouts  3.4 us (11%)
    pallas_call x1, Pallas kernels, per_device(): pl.pallas_call(functools.partial(kernel, n_tm, n_as), out_shape=vmem((fie...  27.6 us
    unnamed x1, local copies, waits for them, and re-layouts  3.4 us

profile of v5, /device:TPU:1, one launch (start us, length us, event | category | flops | bytes accessed | tf_op | source)
XLA Modules:
  0.0 31.0 jit_solution(14907044068062497224)
XLA Ops:
  0.0 27.6 %shard_map.37 = f32[4,256,2048]{2,1,0:T(8,128)S(1)} custom-call(f32[4,256,2048]{2,1,0:T(8,128)} %values.1, s32[1,2048]{1,0:T(1,128)} %bitcast.2, s32[1,2048]{1,0:T(1,128)} %bitcast.3), custom_call_target="tpu_custom_call" | custom-call | tf_op jit(solution)/shard_map/pallas_call | solution.py:516
  27.6 3.4 %copy.5 = f32[4,256,2048]{2,1,0:T(8,128)} copy(f32[4,256,2048]{2,1,0:T(8,128)S(1)} %shard_map.37) | data formatting | bytes 16777216

commit v6 on v5

--- a/solution.py
+++ b/solution.py
@@ -13,7 +13,8 @@
 CLIP = 3.0
 ROLL_UNROLL = 4
 UNROLL = 4
-HELD = 1
+HELD = 0
+CUTS = 4
 
 
 def field_groups(fields):
@@ -21,14 +22,30 @@
     return [(start, min(half, fields - start)) for start in range(0, fields, half)]
 
 
-def halo_pieces(fields, chunks):
-    pieces = [(f, 0, chunks) for f in range(fields - 1)]
-    first, left = 0, chunks
-    while left > 0:
-        size = max(left // 2, 1)
-        pieces.append((fields - 1, first, size))
-        first, left = first + size, left - size
+def lane_pieces(chunks, cuts):
+    if cuts and chunks % cuts == 0:
+        size = chunks // cuts
+        return [(c * size, size) for c in range(cuts)]
+    if cuts:
+        return [(0, chunks)]
+    pieces, first = [], 0
+    while first < chunks:
+        size = max((chunks - first) // 2, 1)
+        pieces.append((first, size))
+        first += size
     return pieces
+
+
+def halo_pieces(fields, own, chunks):
+    cuts = [CUTS if f == own - 1 else 1 for f in range(fields)]
+    if fields > own:
+        cuts[fields - 1] = 0
+    return [(f, *piece) for f in range(fields) for piece in lane_pieces(chunks, cuts[f])]
+
+
+def back_pieces(fields, own, chunks):
+    cuts = [CUTS if f == fields - 1 else 1 for f in range(fields)]
+    return [(f, *piece) for f in range(own, fields) for piece in lane_pieces(chunks, cuts[f])]
 
 
 def greeting_rounds(n):
@@ -41,7 +58,7 @@
     n_tm, n_as, values, opened_hbm, closed_hbm, out,
     x, rolling, weight, inverse, opened_ref, closed_ref,
     acc, columns_of, part, got, totals, counts, advice, advised,
-    load_sem, halo_send, halo_recv, back_send, back_recv, advice_sem, send_sem, recv_sem, hello,
+    load_sem, halo_send, halo_recv, back_send, back_recv, advice_send, advice_recv, send_sem, recv_sem, hello,
 ):
     fields, rows, assets = values.shape
     blocks = rows // WINDOW
@@ -105,9 +122,9 @@
     for copy in dates + loads:
         copy.start()
 
-    pieces = halo_pieces(fields, chunks)
+    landing = {f: [] for f in range(fields)}
     halos = []
-    for i, (f, first, size) in enumerate(pieces):
+    for i, (f, first, size) in enumerate(halo_pieces(fields, own, chunks)):
         cols = pl.ds(first * LANES, size * LANES)
         halos.append(pltpu.make_async_remote_copy(
             src_ref=values.at[f, pl.ds(rows - WINDOW, WINDOW), cols],
@@ -116,27 +133,34 @@
             recv_sem=halo_recv.at[i],
             device_id={"tm": later},
         ))
-    backs = [
+        landing[f].append((halos[-1], first, size))
+    returning = {f: [] for f in range(own, fields)}
+    backs = []
+    for i, (f, first, size) in enumerate(back_pieces(fields, own, chunks)):
+        cols = pl.ds(first * LANES, size * LANES)
+        backs.append(pltpu.make_async_remote_copy(
+            src_ref=values.at[f, pl.ds(0, WINDOW), cols],
+            dst_ref=x.at[f, pl.ds(WINDOW + rows, WINDOW), cols],
+            send_sem=back_send.at[i],
+            recv_sem=back_recv.at[i],
+            device_id={"tm": before},
+        ))
+        returning[f].append((backs[-1], first, size))
+    advising = [
         pltpu.make_async_remote_copy(
-            src_ref=values.at[f, pl.ds(0, WINDOW)],
-            dst_ref=x.at[f, pl.ds(WINDOW + rows, WINDOW), pl.ds(0, assets)],
-            send_sem=back_send.at[f - own],
-            recv_sem=back_recv.at[f - own],
-            device_id={"tm": before},
+            src_ref=advice.at[u],
+            dst_ref=advised.at[u],
+            send_sem=advice_send.at[u],
+            recv_sem=advice_recv.at[u],
+            device_id={"tm": later},
         )
-        for f in range(own, fields)
+        for u in range(helped)
     ]
-    advising = pltpu.make_async_remote_copy(
-        src_ref=advice,
-        dst_ref=advised,
-        send_sem=advice_sem.at[0],
-        recv_sem=advice_sem.at[1],
-        device_id={"tm": later},
-    )
-    free = len(halos) - min(HELD, len(halos) - (fields - 1))
+    free = len(halos) - min(HELD, len(landing[fields - 1]) - 1)
+    odd = lax.rem(tm, 2) == 1
 
     def rows_of(slot):
-        return pl.ds(0, 2 * own if slot >= tail else stats)
+        return pl.ds(0, 2 if slot >= tail else stats)
 
     def send(slot):
         for d in range(1, n_as):
@@ -172,18 +196,37 @@
     def column_pair(i):
         return columns_of[i, :WINDOW, :], columns_of[i, WINDOW:, :]
 
+    pl.semaphore_wait(barrier, expected)
+
+    @pl.when(has_prev & ~odd)
+    def _():
+        for copy in backs:
+            copy.start()
+
+    @pl.when(has_next)
+    def _():
+        for copy in halos[:free]:
+            copy.start()
+
+    @pl.when(has_prev & odd)
+    def _():
+        for copy in backs:
+            copy.start()
+
     zero = jnp.zeros((WINDOW, LANES), jnp.float32)
-    part[...] = jnp.zeros(part.shape, part.dtype)
-    acc[...] = jnp.zeros(acc.shape, acc.dtype)
     first_stamp = tm * rows - WINDOW
-    for copy in dates:
-        copy.wait()
-
-    @pl.when(tm == 0)
-    def _():
-        @pl.loop(0, fields)
-        def clear(f):
-            x[f, pl.ds(0, WINDOW), pl.ds(0, assets)] = jnp.zeros((WINDOW, assets), jnp.float32)
+
+    def start_listing():
+        part[...] = jnp.zeros(part.shape, part.dtype)
+        acc[...] = jnp.zeros(acc.shape, acc.dtype)
+        for copy in dates:
+            copy.wait()
+
+        @pl.when(tm == 0)
+        def _():
+            @pl.loop(0, fields)
+            def clear(f):
+                x[f, pl.ds(0, WINDOW), pl.ds(0, assets)] = jnp.zeros((WINDOW, assets), jnp.float32)
 
     def listing(b):
         start = pl.multiple_of(b * WINDOW, WINDOW)
@@ -211,30 +254,24 @@
         pl.loop(low, high)(listing)
 
     ahead = min(2, blocks)
-    listing_blocks(0, ahead)
-    pl.semaphore_wait(barrier, expected)
-
-    for i in range(free):
-        @pl.when(has_next)
-        def _():
-            halos[i].start()
-
-        if i < helped:
-            @pl.when(has_prev)
-            def _():
-                backs[i].start()
 
     for r in range(rounds):
         greet(hello.at[r])
         if r == 0:
+            start_listing()
+            listing_blocks(0, ahead)
+        if r == 1:
             listing_blocks(ahead, blocks)
-        if r == 1:
+        if r == 2:
             listing_blocks(blocks, blocks + 2)
         if r < rounds - 1:
             pl.semaphore_wait(hello.at[r], near)
     if rounds < 1:
+        start_listing()
+        listing_blocks(0, ahead)
+    if rounds < 2:
         listing_blocks(ahead, blocks)
-    if rounds < 2:
+    if rounds < 3:
         listing_blocks(blocks, blocks + 2)
     reduce_items(0, blocks + 1)
 
@@ -262,7 +299,7 @@
         ending = jnp.concatenate([sums[j] for j in range(tiles, 2 * tiles)], axis=0)
         return ending * inverse[pl.ds(top + WINDOW, WINDOW), cols]
 
-    def roll_window(f, b, i):
+    def roll_window(f, b, i, low=0, size=chunks):
         top = pl.multiple_of(b * WINDOW, WINDOW)
 
         def chunk(c, carry):
@@ -270,7 +307,10 @@
             rolling[f, pl.ds(top, WINDOW), columns(c)] = means
             return carry[0] + means, carry[1] + means * means
 
-        first, second = lax.fori_loop(0, chunks, chunk, (zero, zero), unroll=ROLL_UNROLL)
+        carry = (zero, zero) if low == 0 else (acc[i, :WINDOW, :], acc[i, WINDOW:, :])
+        first, second = lax.fori_loop(
+            low, low + size, chunk, carry, unroll=min(ROLL_UNROLL, size)
+        )
         acc[i, :WINDOW, :] = first
         acc[i, WINDOW:, :] = second
 
@@ -316,7 +356,7 @@
     def score_finish(f, low, size, i):
         first, second = column_pair(i), column_pair(i + 1)
 
-        @pl.loop(low, low + size, unroll=min(2, size))
+        @pl.loop(low, low + size, unroll=min(UNROLL, size))
         def chunk(c):
             cols = columns(c)
             out[f, :WINDOW, cols] = standardized(rolling[f, :WINDOW, cols], cols, first, second)
@@ -378,17 +418,21 @@
         def item(i):
             finish(start + lax.rem(i, size), lax.div(i, size), i)
 
+    def tail_own(u):
+        for copy, low, size in landing[u]:
+            copy.wait_recv()
+            roll_window(u, 0, stats + 2 * u, low, size)
+
+    def tail_help(u):
+        for copy, low, size in returning[own + u]:
+            copy.wait_recv()
+            roll_window(own + u, blocks, stats + 2 * u + 1, low, size)
+
     def tail_first(u):
-        @pl.when(has_prev)
-        def _():
-            halos[u].wait_recv()
-            roll_window(u, 0, stats + 2 * u)
-
+        pl.when(has_prev & odd)(functools.partial(tail_own, u))
         if u < helped:
-            @pl.when(has_next)
-            def _():
-                backs[u].wait_recv()
-                roll_window(own + u, blocks, stats + 2 * u + 1)
+            pl.when(has_next)(functools.partial(tail_help, u))
+        pl.when(has_prev & ~odd)(functools.partial(tail_own, u))
 
     def tail_second(u):
         @pl.when(has_prev)
@@ -400,101 +444,133 @@
             def _():
                 clip_scores(own + u, blocks, stats + 2 * u + 1)
 
-    def tail_exchange():
-        reduce_items(tail, 2 * own, stats)
-        send(tail)
-
-    def tail_scores():
-        receive(tail)
-        spread_items(totals[tail], counts[last], 2 * own, stats)
-        for u in range(own):
-            tail_second(u)
-        reduce_items(tail + 1, 2 * own, stats)
-        send(tail + 1)
-
+    def tail_exchange(u):
+        reduce_items(tail + 2 * u, 2, stats + 2 * u)
+        send(tail + 2 * u)
+
+    def tail_scores(u):
+        slot = tail + 2 * u
+        receive(slot)
+        spread_items(totals[slot], counts[last], 2, stats + 2 * u)
+        tail_second(u)
+        reduce_items(slot + 1, 2, stats + 2 * u)
+        send(slot + 1)
+
+    def tail_last(u):
+        slot = tail + 2 * u
+        receive(slot + 1)
+        if u < helped:
+            advice[u, :1, :] = totals[slot, 1:2, :]
+            advice[u, 1:2, :] = totals[slot + 1, 1:2, :]
+
+            @pl.when(has_next)
+            def _():
+                advising[u].start()
+
+        @pl.when(has_prev)
+        def _():
+            spread_items(totals[slot + 1], counts[last], 1, stats + 2 * u)
+            finish(u, 0, stats + 2 * u)
+
+    def split_pieces(f):
+        held = len(halos) - free if f == fields - 1 else 0
+        return landing[f][:len(landing[f]) - held], landing[f][len(landing[f]) - held:]
+
+    def last_rolls(u):
+        for copy, low, size in split_pieces(own + u)[0]:
+            copy.wait_recv()
+            roll_only(own + u, low, size)
+
+    def last_fields():
+        count = jnp.broadcast_to(counts[last, :1, :], advised.shape[1:])
+        for u in range(helped):
+            advising[u].wait_recv()
+            spread_items(advised[u], count, 2, 2 * u)
+        for u in range(helped):
+            rolled, landed = split_pieces(own + u)
+            score_finish(own + u, 0, sum(size for _, _, size in rolled), 2 * u)
+            for copy, low, size in landed:
+                copy.wait_recv()
+                roll_finish(own + u, low, size, 2 * u)
+
+    late = own - 1
     for g in range(len(groups)):
         main_first(g)
-    tail_first(0)
+    for u in range(late):
+        tail_first(u)
+        tail_exchange(u)
 
     @pl.when(tm == 0)
     def _():
-        for u in range(1, own):
-            tail_first(u)
-        tail_exchange()
+        tail_first(late)
+        tail_exchange(late)
 
     receive(0)
-    for i in range(2 * own):
-        b = 0 if i % 2 == 0 else blocks
+    for i in range(2):
+        b = 0 if i == 0 else blocks
         counts[last, i:i + 1, :] = jnp.maximum(totals[0, b:b + 1, :], 1.0)
     main_counts(0)
     main_second(0)
 
     @pl.when(has_prev)
     def _():
-        for u in range(1, own):
-            tail_first(u)
-        tail_exchange()
+        tail_first(late)
+        tail_exchange(late)
 
     for g in range(1, len(groups)):
         main_counts(g)
         main_second(g)
+    for u in range(late):
+        tail_scores(u)
 
     @pl.when(tm == 0)
     def _():
-        tail_scores()
+        tail_scores(late)
 
     for g in range(len(groups) - 1):
         main_third(g)
 
     @pl.when(has_prev)
     def _():
-        tail_scores()
-
-    main_third(len(groups) - 1)
-    landing = list(zip(halos, pieces))[own:]
-    early = landing[:len(landing) - (len(halos) - free)]
-    sooner = [entry for entry in early if entry[1][0] < fields - 1]
+        tail_scores(late)
 
     @pl.when(has_prev)
     def _():
-        for copy, (f, low, size) in sooner:
-            copy.wait_recv()
-            roll_only(f, low, size)
-
-    receive(tail + 1)
-    for u in range(helped):
-        i = 2 * u
-        advice[i:i + 1, :] = totals[tail, i + 1:i + 2, :]
-        advice[i + 1:i + 2, :] = totals[tail + 1, i + 1:i + 2, :]
+        main_third(len(groups) - 1)
+
+    for u in range(late):
+        tail_last(u)
+
+    @pl.when(has_prev)
+    def _():
+        for u in range(helped - 1):
+            last_rolls(u)
+
+    tail_last(late)
 
     @pl.when(has_next)
     def _():
-        advising.start()
         for copy in halos[free:]:
             copy.start()
 
+    @pl.when(tm == 0)
+    def _():
+        main_third(len(groups) - 1)
+
     @pl.when(has_prev)
     def _():
-        spread_items(totals[tail + 1], counts[last], 2 * own)
-        for u in range(own):
-            finish(u, 0, 2 * u)
-        for copy, (f, low, size) in early[len(sooner):]:
-            copy.wait_recv()
-            roll_only(f, low, size)
-        advising.wait_recv()
-        spread_items(advised[...], jnp.broadcast_to(counts[last, :1, :], advised.shape), 2 * helped)
-        for copy, (f, low, size) in early:
-            score_finish(f, low, size, 2 * (f - own))
-        for copy, (f, low, size) in landing[len(early):]:
-            copy.wait_recv()
-            roll_finish(f, low, size, 2 * (f - own))
+        for u in range(helped - 1, helped):
+            last_rolls(u)
+        last_fields()
+
+    @pl.when(has_prev)
+    def _():
         for copy in backs:
             copy.wait_send()
 
     @pl.when(has_next)
     def _():
-        advising.wait_send()
-        for copy in halos:
+        for copy in advising + halos:
             copy.wait_send()
 
     for slot in range(part.shape[0]):
@@ -507,9 +583,10 @@
     blocks = rows // WINDOW
     groups = field_groups(fields)
     own = groups[0][1]
-    stats = -(-max(own * blocks, blocks + 2, 2 * own) // SUBLANES) * SUBLANES
-    slots = 1 + 2 * len(groups) + 2
-    cuts = len(halo_pieces(fields, assets // LANES))
+    stats = -(-max(own * blocks, blocks + 2) // SUBLANES) * SUBLANES
+    slots = 1 + 2 * len(groups) + 2 * own
+    cuts = len(halo_pieces(fields, own, assets // LANES))
+    back_cuts = max(len(back_pieces(fields, own, assets // LANES)), 1)
     f32 = jnp.float32
     vmem = pltpu.VMEM
     dma = pltpu.SemaphoreType.DMA
@@ -531,14 +608,15 @@
             vmem((slots, n_as - 1, stats, LANES), f32),
             vmem((slots, stats, LANES), f32),
             vmem((len(groups) + 1, stats, LANES), f32),
-            vmem((stats, LANES), f32),
-            vmem((stats, LANES), f32),
+            vmem((own, SUBLANES, LANES), f32),
+            vmem((own, SUBLANES, LANES), f32),
             dma((fields + 2,)),
             dma((cuts,)),
             dma((cuts,)),
+            dma((back_cuts,)),
+            dma((back_cuts,)),
             dma((own,)),
             dma((own,)),
-            dma((2,)),
             dma((slots,)),
             dma((slots,)),
             pltpu.SemaphoreType.REGULAR((max(greeting_rounds(n_as), 1),)),

time: 31.2 us -> 30.9 us (level)
  no operation moved by 1% of the time
where the time goes in v6:
time: 30.9 us; the launch traced here: 30.8 us
  Pallas kernels  27.3 us (88%)
  local copies, waits for them, and re-layouts  3.4 us (11%)
    pallas_call x1, Pallas kernels, per_device(): pl.pallas_call(functools.partial(kernel, n_tm, n_as), out_shape=vmem((fie...  27.3 us
    unnamed x1, local copies, waits for them, and re-layouts  3.4 us

profile of v6, /device:TPU:1, one launch (start us, length us, event | category | flops | bytes accessed | tf_op | source)
XLA Modules:
  0.0 30.8 jit_solution(15188721780474042108)
XLA Ops:
  0.0 27.3 %shard_map.37 = f32[4,256,2048]{2,1,0:T(8,128)S(1)} custom-call(f32[4,256,2048]{2,1,0:T(8,128)} %values.1, s32[1,2048]{1,0:T(1,128)} %bitcast.2, s32[1,2048]{1,0:T(1,128)} %bitcast.3), custom_call_target="tpu_custom_call" | custom-call | tf_op jit(solution)/shard_map/pallas_call | solution.py:593
  27.4 3.4 %copy.5 = f32[4,256,2048]{2,1,0:T(8,128)} copy(f32[4,256,2048]{2,1,0:T(8,128)S(1)} %shard_map.37) | data formatting | bytes 16777216

commit v7 on v6

--- a/solution.py
+++ b/solution.py
@@ -13,7 +13,6 @@
 CLIP = 3.0
 ROLL_UNROLL = 4
 UNROLL = 4
-HELD = 0
 CUTS = 4
 
 
@@ -54,10 +53,25 @@
     return max(n // 2 - 1, 0)
 
 
+def spread(columns_of, sums, count, items, first=0):
+    mean = sums / count
+    other = pltpu.roll(mean, WINDOW, 1)
+    scale = 1.0 / jnp.sqrt(jnp.maximum(mean - other * other, 0.0) + 0.1)
+    lane = lax.broadcasted_iota(jnp.int32, mean.shape, 1)
+    row = jnp.where(lane < WINDOW, mean, scale)
+    for i in range(items):
+        columns_of[first + i] = jnp.broadcast_to(row[i:i + 1], (LANES, LANES)).T
+
+
+def chunk_columns(c):
+    return pl.ds(pl.multiple_of(c * LANES, LANES), LANES)
+
+
 def kernel(
-    n_tm, n_as, values, opened_hbm, closed_hbm, out,
+    n_tm, n_as, values, opened_hbm, closed_hbm,
+    out, rolled, head_weight, advised, head_count,
     x, rolling, weight, inverse, opened_ref, closed_ref,
-    acc, columns_of, part, got, totals, counts, advice, advised,
+    acc, columns_of, part, got, totals, counts, advice,
     load_sem, halo_send, halo_recv, back_send, back_recv, advice_send, advice_recv, send_sem, recv_sem, hello,
 ):
     fields, rows, assets = values.shape
@@ -156,7 +170,6 @@
         )
         for u in range(helped)
     ]
-    free = len(halos) - min(HELD, len(landing[fields - 1]) - 1)
     odd = lax.rem(tm, 2) == 1
 
     def rows_of(slot):
@@ -177,21 +190,12 @@
         pltpu.make_async_copy(arrived, arrived, recv_sem.at[slot]).wait()
         totals[slot] = part[slot] + jnp.sum(got[slot], axis=0)
 
-    def columns(c):
-        return pl.ds(pl.multiple_of(c * LANES, LANES), LANES)
-
     def reduce_items(slot, items, first=0):
         for i in range(items):
             part[slot, i:i + 1, :] = jnp.sum(acc[first + i].T, axis=0, keepdims=True)
 
     def spread_items(sums, count, items, first=0):
-        mean = sums / count
-        other = pltpu.roll(mean, WINDOW, 1)
-        scale = 1.0 / jnp.sqrt(jnp.maximum(mean - other * other, 0.0) + 0.1)
-        lane = lax.broadcasted_iota(jnp.int32, mean.shape, 1)
-        row = jnp.where(lane < WINDOW, mean, scale)
-        for i in range(items):
-            columns_of[first + i] = jnp.broadcast_to(row[i:i + 1], (LANES, LANES)).T
+        spread(columns_of, sums, count, items, first)
 
     def column_pair(i):
         return columns_of[i, :WINDOW, :], columns_of[i, WINDOW:, :]
@@ -205,7 +209,7 @@
 
     @pl.when(has_next)
     def _():
-        for copy in halos[:free]:
+        for copy in halos:
             copy.start()
 
     @pl.when(has_prev & odd)
@@ -234,7 +238,7 @@
         passed = (first_stamp + start + 1 + row).astype(jnp.float32)
 
         def chunk(c, total):
-            cols = columns(c)
+            cols = chunk_columns(c)
             opened = jnp.maximum(opened_ref[:, cols], 0).astype(jnp.float32)
             closed = closed_ref[:, cols].astype(jnp.float32)
             age = passed - opened
@@ -277,7 +281,7 @@
 
     def window_means(f, b, c):
         top = pl.multiple_of(b * WINDOW, WINDOW)
-        cols = columns(c)
+        cols = chunk_columns(c)
         sublane = lax.broadcasted_iota(jnp.int32, (SUBLANES, LANES), 0)
 
         ends = range(2 * tiles)
@@ -304,7 +308,7 @@
 
         def chunk(c, carry):
             means = window_means(f, b, c)
-            rolling[f, pl.ds(top, WINDOW), columns(c)] = means
+            rolling[f, pl.ds(top, WINDOW), chunk_columns(c)] = means
             return carry[0] + means, carry[1] + means * means
 
         carry = (zero, zero) if low == 0 else (acc[i, :WINDOW, :], acc[i, WINDOW:, :])
@@ -319,7 +323,7 @@
         center, scale = column_pair(i)
 
         def chunk(c, carry):
-            cols = columns(c)
+            cols = chunk_columns(c)
             here = pl.ds(top, WINDOW)
             scored = (rolling[f, here, cols] - center) * scale
             clipped = jnp.minimum(jnp.maximum(scored, -CLIP), CLIP)
@@ -337,37 +341,18 @@
 
         @pl.loop(0, chunks, unroll=UNROLL)
         def chunk(c):
-            cols = columns(c)
+            cols = chunk_columns(c)
             here = pl.ds(top, WINDOW)
             deviate = (rolling[f, here, cols] - middle) * weight[pl.ds(top + WINDOW, WINDOW), cols]
             out[f, here, cols] = deviate * factor
 
-    def standardized(means, cols, first, second):
-        center, scale = first
-        middle, factor = second
-        clipped = jnp.minimum(jnp.maximum((means - center) * scale, -CLIP), CLIP)
-        return (clipped - middle) * weight[WINDOW:2 * WINDOW, cols] * factor
-
-    def roll_only(f, low, size):
+    def roll_only(u, low, size):
         @pl.loop(low, low + size, unroll=min(2, size))
         def chunk(c):
-            rolling[f, :WINDOW, columns(c)] = window_means(f, 0, c)
-
-    def score_finish(f, low, size, i):
-        first, second = column_pair(i), column_pair(i + 1)
-
-        @pl.loop(low, low + size, unroll=min(UNROLL, size))
-        def chunk(c):
-            cols = columns(c)
-            out[f, :WINDOW, cols] = standardized(rolling[f, :WINDOW, cols], cols, first, second)
-
-    def roll_finish(f, low, size, i):
-        first, second = column_pair(i), column_pair(i + 1)
-
-        @pl.loop(low, low + size, unroll=min(2, size))
-        def chunk(c):
-            cols = columns(c)
-            out[f, :WINDOW, cols] = standardized(window_means(f, 0, c), cols, first, second)
+            cols = chunk_columns(c)
+            rolled[u, :, cols] = window_means(own + u, 0, c)
+            if u == 0:
+                head_weight[:, cols] = weight[WINDOW:2 * WINDOW, cols]
 
     def main_items(g):
         size = groups[g][1]
@@ -472,26 +457,10 @@
             spread_items(totals[slot + 1], counts[last], 1, stats + 2 * u)
             finish(u, 0, stats + 2 * u)
 
-    def split_pieces(f):
-        held = len(halos) - free if f == fields - 1 else 0
-        return landing[f][:len(landing[f]) - held], landing[f][len(landing[f]) - held:]
-
     def last_rolls(u):
-        for copy, low, size in split_pieces(own + u)[0]:
+        for copy, low, size in landing[own + u]:
             copy.wait_recv()
-            roll_only(own + u, low, size)
-
-    def last_fields():
-        count = jnp.broadcast_to(counts[last, :1, :], advised.shape[1:])
-        for u in range(helped):
-            advising[u].wait_recv()
-            spread_items(advised[u], count, 2, 2 * u)
-        for u in range(helped):
-            rolled, landed = split_pieces(own + u)
-            score_finish(own + u, 0, sum(size for _, _, size in rolled), 2 * u)
-            for copy, low, size in landed:
-                copy.wait_recv()
-                roll_finish(own + u, low, size, 2 * u)
+            roll_only(u, low, size)
 
     late = own - 1
     for g in range(len(groups)):
@@ -548,11 +517,6 @@
 
     tail_last(late)
 
-    @pl.when(has_next)
-    def _():
-        for copy in halos[free:]:
-            copy.start()
-
     @pl.when(tm == 0)
     def _():
         main_third(len(groups) - 1)
@@ -561,7 +525,9 @@
     def _():
         for u in range(helped - 1, helped):
             last_rolls(u)
-        last_fields()
+        head_count[...] = jnp.broadcast_to(counts[last, :1, :], head_count.shape)
+        for copy in advising:
+            copy.wait_recv()
 
     @pl.when(has_prev)
     def _():
@@ -576,6 +542,54 @@
     for slot in range(part.shape[0]):
         sent = got.at[slot, :, rows_of(slot)]
         pltpu.make_async_copy(sent, sent, send_sem.at[slot]).wait()
+
+
+def finisher(
+    own, out, rolled, head_weight, advised, head_count, result, head, columns_of, sem,
+):
+    fields, rows, assets = out.shape
+    helped = fields - own
+    below = pl.ds(WINDOW, rows - WINDOW)
+    tm = lax.axis_index("tm")
+    copies = [
+        pltpu.make_async_copy(out.at[f, below], result.at[f, below], sem.at[0, f])
+        for f in range(fields)
+    ]
+    done = [
+        pltpu.make_async_copy(out.at[f, :WINDOW], result.at[f, :WINDOW], sem.at[1, f])
+        for f in range(fields)
+    ]
+    finished = [
+        pltpu.make_async_copy(head.at[u], result.at[own + u, :WINDOW], sem.at[1, own + u])
+        for u in range(helped)
+    ]
+    for copy in copies + done[:own]:
+        copy.start()
+
+    @pl.when(tm == 0)
+    def _():
+        for copy in done[own:]:
+            copy.start()
+
+    @pl.when(tm > 0)
+    def _():
+        for u in range(helped):
+            spread(columns_of, advised[u], head_count[...], 2, 2 * u)
+        for u in range(helped):
+            center, scale = columns_of[2 * u, :WINDOW, :], columns_of[2 * u, WINDOW:, :]
+            middle, factor = columns_of[2 * u + 1, :WINDOW, :], columns_of[2 * u + 1, WINDOW:, :]
+
+            @pl.loop(0, assets // LANES, unroll=2)
+            def chunk(c):
+                cols = chunk_columns(c)
+                scored = (rolled[u, :, cols] - center) * scale
+                clipped = jnp.minimum(jnp.maximum(scored, -CLIP), CLIP)
+                head[u, :, cols] = (clipped - middle) * head_weight[:, cols] * factor
+
+            finished[u].start()
+
+    for copy in copies + done:
+        copy.wait()
 
 
 def per_device(n_tm, n_as, values, listed_from, listed_until):
@@ -590,11 +604,20 @@
     f32 = jnp.float32
     vmem = pltpu.VMEM
     dma = pltpu.SemaphoreType.DMA
-    return pl.pallas_call(
+    helped = max(fields - own, 1)
+    parts = (
+        vmem((fields, rows, assets), f32),
+        vmem((helped, WINDOW, assets + LANES), f32),
+        vmem((WINDOW, assets + LANES), f32),
+        vmem((own, SUBLANES, LANES), f32),
+        vmem((SUBLANES, LANES), f32),
+    )
+    in_vmem = [pl.BlockSpec(memory_space=vmem)] * len(parts)
+    outputs = pl.pallas_call(
         functools.partial(kernel, n_tm, n_as),
-        out_shape=vmem((fields, rows, assets), f32),
+        out_shape=parts,
         in_specs=[pl.BlockSpec(memory_space=pltpu.HBM)] * 3,
-        out_specs=pl.BlockSpec(memory_space=vmem),
+        out_specs=in_vmem,
         scratch_shapes=[
             vmem((fields, WINDOW + rows + WINDOW, assets + LANES), f32),
             vmem((fields, rows + WINDOW, assets + LANES), f32),
@@ -608,7 +631,6 @@
             vmem((slots, n_as - 1, stats, LANES), f32),
             vmem((slots, stats, LANES), f32),
             vmem((len(groups) + 1, stats, LANES), f32),
-            vmem((own, SUBLANES, LANES), f32),
             vmem((own, SUBLANES, LANES), f32),
             dma((fields + 2,)),
             dma((cuts,)),
@@ -625,6 +647,18 @@
             collective_id=0, has_side_effects=True, vmem_limit_bytes=48 * 2**20
         ),
     )(values, listed_from[None], listed_until[None])
+    return pl.pallas_call(
+        functools.partial(finisher, own),
+        out_shape=jax.ShapeDtypeStruct((fields, rows, assets), f32),
+        in_specs=in_vmem,
+        out_specs=pl.BlockSpec(memory_space=pltpu.HBM),
+        scratch_shapes=[
+            vmem((helped, WINDOW, assets), f32),
+            vmem((2 * own, LANES, LANES), f32),
+            dma((2, fields)),
+        ],
+        compiler_params=pltpu.CompilerParams(vmem_limit_bytes=4 * 2**20),
+    )(*outputs)
 
 
 def solution(mesh):

time: 30.9 us -> 30.6 us (level); the launches traced: 30.8 us -> 30.1 us
  local copies, waits for them, and re-layouts: 3.4 us -> 0 us
  Pallas kernels: 27.3 us -> 30.1 us
    unnamed x1 -> x0, local copies, waits for them, and re-layouts: 3.4 us -> none
    pallas_call x1 -> x2, Pallas kernels: 27.3 us -> 30.1 us  [the longest x1 26.7 us: per_device(): pl.pallas_call(functools.partial(kernel, n_tm, n_as), out_shape=parts, in...]
where the time goes in v7:
time: 30.6 us; the launch traced here: 30.1 us
  Pallas kernels  30.1 us (98%)
    pallas_call x1, Pallas kernels, per_device(): pl.pallas_call(functools.partial(kernel, n_tm, n_as), out_shape=parts, in...  26.7 us
    pallas_call x1, Pallas kernels, per_device(): pl.pallas_call(functools.partial(finisher, own), out_shape=jax.ShapeDtype...  3.37 us

profile of v7, /device:TPU:1, one launch (start us, length us, event | category | flops | bytes accessed | tf_op | source)
XLA Modules:
  0.0 30.1 jit_solution(17340674099813607980)
XLA Ops:
  0.0 26.7 %shard_map.37 = (f32[4,256,2048]{2,1,0:T(8,128)S(1)}, f32[2,64,2176]{2,1,0:T(8,128)S(1)}, f32[64,2176]{1,0:T(8,128)S(1)}, f32[2,8,128]{2,1,0:T(8,128)S(1)}, f32[8,128]{1,0:T(8,128)S(1)}) custom-call(f32[4,256,2048]{2,1,0:T(8,128)} %values.1, s32[1,2048]{1,0:T(1,128)} %bitcast.2, s32[1,2048]{1,0:T(1,128)} %bitcast.3), custom_call_target="tpu_custom_call" | custom-call | tf_op jit(solution)/shard_map/pallas_call | solution.py:616
  26.7 3.4 %shard_map.38 = f32[4,256,2048]{2,1,0:T(8,128)} custom-call(f32[4,256,2048]{2,1,0:T(8,128)S(1)} %get-tuple-element.10.out, f32[2,64,2176]{2,1,0:T(8,128)S(1)} %get-tuple-element.11.rolled, f32[64,2176]{1,0:T(8,128)S(1)} %get-tuple-element.12.head_weight, f32[2,8,128]{2,1,0:T(8,128)S(1)} %get-tuple-element.13.advised, f32[8,128]{1,0:T(8,128)S(1)} %get-tuple-element.14.head_count), custom_call_target="tpu_custom_call" | custom-call | tf_op jit(solution)/shard_map/pallas_call | solution.py:650

commit v8 on v7

--- a/solution.py
+++ b/solution.py
@@ -11,7 +11,7 @@
 LANES = 128
 SUBLANES = 8
 CLIP = 3.0
-ROLL_UNROLL = 4
+ROLL_UNROLL = 8
 UNROLL = 4
 CUTS = 4
 
@@ -21,30 +21,21 @@
     return [(start, min(half, fields - start)) for start in range(0, fields, half)]
 
 
-def lane_pieces(chunks, cuts):
-    if cuts and chunks % cuts == 0:
+def lane_pieces(fields, split, chunks):
+    pieces = []
+    for f in fields:
+        cuts = CUTS if f in split and chunks % CUTS == 0 else 1
         size = chunks // cuts
-        return [(c * size, size) for c in range(cuts)]
-    if cuts:
-        return [(0, chunks)]
-    pieces, first = [], 0
-    while first < chunks:
-        size = max((chunks - first) // 2, 1)
-        pieces.append((first, size))
-        first += size
+        pieces += [(f, c * size, size) for c in range(cuts)]
     return pieces
 
 
 def halo_pieces(fields, own, chunks):
-    cuts = [CUTS if f == own - 1 else 1 for f in range(fields)]
-    if fields > own:
-        cuts[fields - 1] = 0
-    return [(f, *piece) for f in range(fields) for piece in lane_pieces(chunks, cuts[f])]
+    return lane_pieces(range(fields), (own - 1, fields - 1), chunks)
 
 
 def back_pieces(fields, own, chunks):
-    cuts = [CUTS if f == fields - 1 else 1 for f in range(fields)]
-    return [(f, *piece) for f in range(own, fields) for piece in lane_pieces(chunks, cuts[f])]
+    return lane_pieces(range(own, fields), (fields - 1,), chunks)
 
 
 def greeting_rounds(n):
@@ -72,7 +63,7 @@
     out, rolled, head_weight, advised, head_count,
     x, rolling, weight, inverse, opened_ref, closed_ref,
     acc, columns_of, part, got, totals, counts, advice,
-    load_sem, halo_send, halo_recv, back_send, back_recv, advice_send, advice_recv, send_sem, recv_sem, hello,
+    load_sem, sent_sem, halo_recv, back_recv, recv_sem, hello,
 ):
     fields, rows, assets = values.shape
     blocks = rows // WINDOW
@@ -91,13 +82,16 @@
     has_next = tm < n_tm - 1
     has_prev = tm > 0
 
+    def wait_for(ref, semaphore):
+        pltpu.make_async_copy(ref, ref, semaphore).wait()
+
     dates = [
-        pltpu.make_async_copy(opened_hbm, opened_ref, load_sem.at[fields]),
-        pltpu.make_async_copy(closed_hbm, closed_ref, load_sem.at[fields + 1]),
+        pltpu.make_async_copy(opened_hbm, opened_ref, load_sem.at[len(groups)]),
+        pltpu.make_async_copy(closed_hbm, closed_ref, load_sem.at[len(groups) + 1]),
     ]
     loads = [
         pltpu.make_async_copy(
-            values.at[f], x.at[f, pl.ds(WINDOW, rows), pl.ds(0, assets)], load_sem.at[f]
+            values.at[f], x.at[f, pl.ds(WINDOW, rows), pl.ds(0, assets)], load_sem.at[f // own]
         )
         for f in range(fields)
     ]
@@ -143,7 +137,7 @@
         halos.append(pltpu.make_async_remote_copy(
             src_ref=values.at[f, pl.ds(rows - WINDOW, WINDOW), cols],
             dst_ref=x.at[f, pl.ds(0, WINDOW), cols],
-            send_sem=halo_send.at[i],
+            send_sem=sent_sem.at[0],
             recv_sem=halo_recv.at[i],
             device_id={"tm": later},
         ))
@@ -155,7 +149,7 @@
         backs.append(pltpu.make_async_remote_copy(
             src_ref=values.at[f, pl.ds(0, WINDOW), cols],
             dst_ref=x.at[f, pl.ds(WINDOW + rows, WINDOW), cols],
-            send_sem=back_send.at[i],
+            send_sem=sent_sem.at[1],
             recv_sem=back_recv.at[i],
             device_id={"tm": before},
         ))
@@ -164,8 +158,8 @@
         pltpu.make_async_remote_copy(
             src_ref=advice.at[u],
             dst_ref=advised.at[u],
-            send_sem=advice_send.at[u],
-            recv_sem=advice_recv.at[u],
+            send_sem=sent_sem.at[2],
+            recv_sem=sent_sem.at[3],
             device_id={"tm": later},
         )
         for u in range(helped)
@@ -180,14 +174,14 @@
             pltpu.make_async_remote_copy(
                 src_ref=part.at[slot, rows_of(slot)],
                 dst_ref=got.at[slot, d - 1, rows_of(slot)],
-                send_sem=send_sem.at[slot],
+                send_sem=sent_sem.at[5 if slot >= tail else 4],
                 recv_sem=recv_sem.at[slot],
                 device_id={"asset": lax.rem(me + d, n_as)},
             ).start()
 
     def receive(slot):
         arrived = got.at[slot, :, rows_of(slot)]
-        pltpu.make_async_copy(arrived, arrived, recv_sem.at[slot]).wait()
+        wait_for(arrived, recv_sem.at[slot])
         totals[slot] = part[slot] + jnp.sum(got[slot], axis=0)
 
     def reduce_items(slot, items, first=0):
@@ -199,23 +193,6 @@
 
     def column_pair(i):
         return columns_of[i, :WINDOW, :], columns_of[i, WINDOW:, :]
-
-    pl.semaphore_wait(barrier, expected)
-
-    @pl.when(has_prev & ~odd)
-    def _():
-        for copy in backs:
-            copy.start()
-
-    @pl.when(has_next)
-    def _():
-        for copy in halos:
-            copy.start()
-
-    @pl.when(has_prev & odd)
-    def _():
-        for copy in backs:
-            copy.start()
 
     zero = jnp.zeros((WINDOW, LANES), jnp.float32)
     first_stamp = tm * rows - WINDOW
@@ -257,26 +234,45 @@
     def listing_blocks(low, high):
         pl.loop(low, high)(listing)
 
-    ahead = min(2, blocks)
-
-    for r in range(rounds):
-        greet(hello.at[r])
-        if r == 0:
-            start_listing()
-            listing_blocks(0, ahead)
-        if r == 1:
-            listing_blocks(ahead, blocks)
-        if r == 2:
-            listing_blocks(blocks, blocks + 2)
-        if r < rounds - 1:
-            pl.semaphore_wait(hello.at[r], near)
-    if rounds < 1:
+    @pl.when(tm == 0)
+    def _():
         start_listing()
-        listing_blocks(0, ahead)
-    if rounds < 2:
-        listing_blocks(ahead, blocks)
-    if rounds < 3:
-        listing_blocks(blocks, blocks + 2)
+        listing_blocks(0, blocks)
+
+    pl.semaphore_wait(barrier, expected)
+
+    @pl.when(has_prev & ~odd)
+    def _():
+        for copy in backs:
+            copy.start()
+
+    @pl.when(has_next)
+    def _():
+        for copy in halos:
+            copy.start()
+
+    @pl.when(has_prev & odd)
+    def _():
+        for copy in backs:
+            copy.start()
+
+    if rounds:
+        greet(hello.at[0])
+
+    @pl.when(has_prev)
+    def _():
+        start_listing()
+        listing_blocks(0, blocks)
+
+    listing_blocks(blocks, blocks + 2)
+
+    def next_round(r):
+        pl.semaphore_wait(hello.at[r], near)
+        if r + 1 < rounds:
+            greet(hello.at[r + 1])
+
+    for r in range(rounds - 2):
+        next_round(r)
     reduce_items(0, blocks + 1)
 
     def window_means(f, b, c):
@@ -360,17 +356,19 @@
 
     def main_first(g):
         start, size = groups[g]
-        for f in range(start, start + size):
-            loads[f].wait()
+        block = x.at[pl.ds(start, size), pl.ds(WINDOW, rows), pl.ds(0, assets)]
+        wait_for(block, load_sem.at[g])
 
         @main_items(g)
         def item(i):
             roll_window(start + lax.rem(i, size), lax.div(i, size), i)
+            if g == 0 and rounds > 1:
+                pl.when(i == (size + size * blocks) // 2)(lambda: next_round(rounds - 2))
 
         reduce_items(1 + 2 * g, size * blocks)
         if g == 0:
             if rounds:
-                pl.semaphore_wait(hello.at[rounds - 1], near)
+                next_round(rounds - 1)
             send(0)
         send(1 + 2 * g)
 
@@ -526,22 +524,21 @@
         for u in range(helped - 1, helped):
             last_rolls(u)
         head_count[...] = jnp.broadcast_to(counts[last, :1, :], head_count.shape)
-        for copy in advising:
-            copy.wait_recv()
-
-    @pl.when(has_prev)
-    def _():
-        for copy in backs:
-            copy.wait_send()
+        wait_for(advised.at[pl.ds(0, helped)], sent_sem.at[3])
+
+    head_rows = pl.ds(0, WINDOW)
+
+    @pl.when(has_prev)
+    def _():
+        wait_for(x.at[pl.ds(own, helped), head_rows, pl.ds(0, assets)], sent_sem.at[1])
 
     @pl.when(has_next)
     def _():
-        for copy in advising + halos:
-            copy.wait_send()
-
-    for slot in range(part.shape[0]):
-        sent = got.at[slot, :, rows_of(slot)]
-        pltpu.make_async_copy(sent, sent, send_sem.at[slot]).wait()
+        wait_for(x.at[:, head_rows, pl.ds(0, assets)], sent_sem.at[0])
+        wait_for(advice.at[pl.ds(0, helped)], sent_sem.at[2])
+
+    wait_for(got.at[pl.ds(0, tail)], sent_sem.at[4])
+    wait_for(got.at[pl.ds(tail, 2 * own), :, pl.ds(0, 2)], sent_sem.at[5])
 
 
 def finisher(
@@ -552,15 +549,15 @@
     below = pl.ds(WINDOW, rows - WINDOW)
     tm = lax.axis_index("tm")
     copies = [
-        pltpu.make_async_copy(out.at[f, below], result.at[f, below], sem.at[0, f])
+        pltpu.make_async_copy(out.at[f, below], result.at[f, below], sem)
         for f in range(fields)
     ]
     done = [
-        pltpu.make_async_copy(out.at[f, :WINDOW], result.at[f, :WINDOW], sem.at[1, f])
+        pltpu.make_async_copy(out.at[f, :WINDOW], result.at[f, :WINDOW], sem)
         for f in range(fields)
     ]
     finished = [
-        pltpu.make_async_copy(head.at[u], result.at[own + u, :WINDOW], sem.at[1, own + u])
+        pltpu.make_async_copy(head.at[u], result.at[own + u, :WINDOW], sem)
         for u in range(helped)
     ]
     for copy in copies + done[:own]:
@@ -588,8 +585,7 @@
 
             finished[u].start()
 
-    for copy in copies + done:
-        copy.wait()
+    pltpu.make_async_copy(out, out, sem).wait()
 
 
 def per_device(n_tm, n_as, values, listed_from, listed_until):
@@ -632,14 +628,10 @@
             vmem((slots, stats, LANES), f32),
             vmem((len(groups) + 1, stats, LANES), f32),
             vmem((own, SUBLANES, LANES), f32),
-            dma((fields + 2,)),
-            dma((cuts,)),
+            dma((len(groups) + 2,)),
+            dma((6,)),
             dma((cuts,)),
             dma((back_cuts,)),
-            dma((back_cuts,)),
-            dma((own,)),
-            dma((own,)),
-            dma((slots,)),
             dma((slots,)),
             pltpu.SemaphoreType.REGULAR((max(greeting_rounds(n_as), 1),)),
         ],
@@ -655,7 +647,7 @@
         scratch_shapes=[
             vmem((helped, WINDOW, assets), f32),
             vmem((2 * own, LANES, LANES), f32),
-            dma((2, fields)),
+            dma(()),
         ],
         compiler_params=pltpu.CompilerParams(vmem_limit_bytes=4 * 2**20),
     )(*outputs)

time: 30.6 us -> 30 us (0.980)
  Pallas kernels: 30.1 us -> 29.7 us
where the time goes in v8:
time: 30 us; the launch traced here: 29.8 us
  Pallas kernels  29.7 us (99%)
    pallas_call x1, Pallas kernels, per_device(): pl.pallas_call(functools.partial(kernel, n_tm, n_as), out_shape=parts, in...  26.4 us
    pallas_call x1, Pallas kernels, per_device(): pl.pallas_call(functools.partial(finisher, own), out_shape=jax.ShapeDtype...  3.3 us

profile of v8, /device:TPU:1, one launch (start us, length us, event | category | flops | bytes accessed | tf_op | source)
XLA Modules:
  0.0 29.8 jit_solution(10266906523246036865)
XLA Ops:
  0.0 26.4 %shard_map.37 = (f32[4,256,2048]{2,1,0:T(8,128)S(1)}, f32[2,64,2176]{2,1,0:T(8,128)S(1)}, f32[64,2176]{1,0:T(8,128)S(1)}, f32[2,8,128]{2,1,0:T(8,128)S(1)}, f32[8,128]{1,0:T(8,128)S(1)}) custom-call(f32[4,256,2048]{2,1,0:T(8,128)} %values.1, s32[1,2048]{1,0:T(1,128)} %bitcast.2, s32[1,2048]{1,0:T(1,128)} %bitcast.3), custom_call_target="tpu_custom_call" | custom-call | tf_op jit(solution)/shard_map/pallas_call | solution.py:612
  26.5 3.3 %shard_map.38 = f32[4,256,2048]{2,1,0:T(8,128)} custom-call(f32[4,256,2048]{2,1,0:T(8,128)S(1)} %get-tuple-element.10.out, f32[2,64,2176]{2,1,0:T(8,128)S(1)} %get-tuple-element.11.rolled, f32[64,2176]{1,0:T(8,128)S(1)} %get-tuple-element.12.head_weight, f32[2,8,128]{2,1,0:T(8,128)S(1)} %get-tuple-element.13.advised, f32[8,128]{1,0:T(8,128)S(1)} %get-tuple-element.14.head_count), custom_call_target="tpu_custom_call" | custom-call | tf_op jit(solution)/shard_map/pallas_call | solution.py:642

commit v9 on v8

--- a/solution.py
+++ b/solution.py
@@ -62,8 +62,8 @@
     n_tm, n_as, values, opened_hbm, closed_hbm,
     out, rolled, head_weight, advised, head_count,
     x, rolling, weight, inverse, opened_ref, closed_ref,
-    acc, columns_of, part, got, totals, counts, advice,
-    load_sem, sent_sem, halo_recv, back_recv, recv_sem, hello,
+    acc, columns_of, packed, part, got, totals, counts, advice,
+    load_sem, sent_sem, halo_recv, top_recv, back_recv, recv_sem, hello,
 ):
     fields, rows, assets = values.shape
     blocks = rows // WINDOW
@@ -130,18 +130,61 @@
     for copy in dates + loads:
         copy.start()
 
+    kept = packed.shape[2] // LANES
     landing = {f: [] for f in range(fields)}
-    halos = []
+    tops = {}
     for i, (f, first, size) in enumerate(halo_pieces(fields, own, chunks)):
         cols = pl.ds(first * LANES, size * LANES)
-        halos.append(pltpu.make_async_remote_copy(
-            src_ref=values.at[f, pl.ds(rows - WINDOW, WINDOW), cols],
-            dst_ref=x.at[f, pl.ds(0, WINDOW), cols],
-            send_sem=sent_sem.at[0],
+        skip = SUBLANES if f else 0
+        copy = pltpu.make_async_remote_copy(
+            src_ref=values.at[f, pl.ds(rows - WINDOW + skip, WINDOW - skip), cols],
+            dst_ref=x.at[f, pl.ds(skip, WINDOW - skip), cols],
+            send_sem=sent_sem.at[6 if f else 0],
             recv_sem=halo_recv.at[i],
             device_id={"tm": later},
-        ))
-        landing[f].append((halos[-1], first, size))
+        )
+        landing[f].append((copy, first, size))
+    for f in range(1, fields):
+        tops[f] = pltpu.make_async_remote_copy(
+            src_ref=packed.at[f - 1],
+            dst_ref=x.at[f, pl.ds(0, SUBLANES), pl.ds(0, kept * LANES)],
+            send_sem=sent_sem.at[7],
+            recv_sem=top_recv.at[f - 1],
+            device_id={"tm": later},
+        )
+
+    def tile_columns(c):
+        return pl.ds(c * LANES, LANES)
+
+    def pack_top(f):
+        sublane = lax.broadcasted_iota(jnp.int32, (SUBLANES, LANES), 0)
+        for c in range(kept):
+            tile = x[f, pl.ds(rows, SUBLANES), tile_columns(c)]
+            if kept < chunks:
+                extra, row = kept + c // (SUBLANES - 1), 1 + c % (SUBLANES - 1)
+                other = x[f, pl.ds(rows, SUBLANES), tile_columns(extra)][row:row + 1]
+                tile = jnp.where(sublane == 0, jnp.broadcast_to(other, tile.shape), tile)
+            packed[f - 1, :, tile_columns(c)] = tile
+
+    def unpack_top(f):
+        if f == 0:
+            return
+        tops[f].wait_recv()
+        sublane = lax.broadcasted_iota(jnp.int32, (SUBLANES, LANES), 0)
+        for extra in range(chunks - kept):
+            tile = jnp.zeros((SUBLANES, LANES), jnp.float32)
+            for k in range(SUBLANES - 1):
+                from_tile = tile_columns((SUBLANES - 1) * extra + k)
+                row = x[f, pl.ds(0, SUBLANES), from_tile][:1]
+                tile = jnp.where(sublane == 1 + k, jnp.broadcast_to(row, tile.shape), tile)
+            x[f, pl.ds(0, SUBLANES), tile_columns(kept + extra)] = tile
+
+    def start_halo(f):
+        if f > 0:
+            tops[f].start()
+        for copy, _, _ in landing[f]:
+            copy.start()
+
     returning = {f: [] for f in range(own, fields)}
     backs = []
     for i, (f, first, size) in enumerate(back_pieces(fields, own, chunks)):
@@ -248,8 +291,7 @@
 
     @pl.when(has_next)
     def _():
-        for copy in halos:
-            copy.start()
+        start_halo(0)
 
     @pl.when(has_prev & odd)
     def _():
@@ -358,12 +400,26 @@
         start, size = groups[g]
         block = x.at[pl.ds(start, size), pl.ds(WINDOW, rows), pl.ds(0, assets)]
         wait_for(block, load_sem.at[g])
+        ahead = [f for f in range(start, start + size) if f > 0]
+
+        @pl.when(has_next)
+        def _():
+            for f in ahead:
+                pack_top(f)
+
+        def middle():
+            @pl.when(has_next)
+            def _():
+                for f in ahead:
+                    start_halo(f)
+
+            if g == 0 and rounds > 1:
+                next_round(rounds - 2)
 
         @main_items(g)
         def item(i):
             roll_window(start + lax.rem(i, size), lax.div(i, size), i)
-            if g == 0 and rounds > 1:
-                pl.when(i == (size + size * blocks) // 2)(lambda: next_round(rounds - 2))
+            pl.when(i == (size + size * blocks) // 2)(middle)
 
         reduce_items(1 + 2 * g, size * blocks)
         if g == 0:
@@ -402,6 +458,7 @@
             finish(start + lax.rem(i, size), lax.div(i, size), i)
 
     def tail_own(u):
+        unpack_top(u)
         for copy, low, size in landing[u]:
             copy.wait_recv()
             roll_window(u, 0, stats + 2 * u, low, size)
@@ -456,6 +513,7 @@
             finish(u, 0, stats + 2 * u)
 
     def last_rolls(u):
+        unpack_top(own + u)
         for copy, low, size in landing[own + u]:
             copy.wait_recv()
             roll_only(u, low, size)
@@ -534,7 +592,11 @@
 
     @pl.when(has_next)
     def _():
-        wait_for(x.at[:, head_rows, pl.ds(0, assets)], sent_sem.at[0])
+        wait_for(x.at[0, head_rows, pl.ds(0, assets)], sent_sem.at[0])
+        if fields > 1:
+            later_rows = pl.ds(SUBLANES, WINDOW - SUBLANES)
+            wait_for(x.at[pl.ds(1, fields - 1), later_rows, pl.ds(0, assets)], sent_sem.at[6])
+            wait_for(packed, sent_sem.at[7])
         wait_for(advice.at[pl.ds(0, helped)], sent_sem.at[2])
 
     wait_for(got.at[pl.ds(0, tail)], sent_sem.at[4])
@@ -601,6 +663,8 @@
     vmem = pltpu.VMEM
     dma = pltpu.SemaphoreType.DMA
     helped = max(fields - own, 1)
+    chunks = assets // LANES
+    kept = chunks - (chunks // SUBLANES if chunks % SUBLANES == 0 else 0)
     parts = (
         vmem((fields, rows, assets), f32),
         vmem((helped, WINDOW, assets + LANES), f32),
@@ -623,14 +687,16 @@
             vmem((1, assets), jnp.int32),
             vmem((stats + 2 * own, LANES, LANES), f32),
             vmem((stats + 2 * own, LANES, LANES), f32),
+            vmem((max(fields - 1, 1), SUBLANES, kept * LANES), f32),
             vmem((slots, stats, LANES), f32),
             vmem((slots, n_as - 1, stats, LANES), f32),
             vmem((slots, stats, LANES), f32),
             vmem((len(groups) + 1, stats, LANES), f32),
             vmem((own, SUBLANES, LANES), f32),
             dma((len(groups) + 2,)),
-            dma((6,)),
+            dma((8,)),
             dma((cuts,)),
+            dma((max(fields - 1, 1),)),
             dma((back_cuts,)),
             dma((slots,)),
             pltpu.SemaphoreType.REGULAR((max(greeting_rounds(n_as), 1),)),

time: 30 us -> 29.8 us (level)
  no operation moved by 1% of the time
where the time goes in v9:
time: 29.8 us; the launch traced here: 29.5 us
  Pallas kernels  29.5 us (99%)
    pallas_call x1, Pallas kernels, per_device(): pl.pallas_call(functools.partial(kernel, n_tm, n_as), out_shape=parts, in...  26.2 us
    pallas_call x1, Pallas kernels, per_device(): pl.pallas_call(functools.partial(finisher, own), out_shape=jax.ShapeDtype...  3.3 us

profile of v9, /device:TPU:1, one launch (start us, length us, event | category | flops | bytes accessed | tf_op | source)
XLA Modules:
  0.0 29.5 jit_solution(2826768520525615329)
XLA Ops:
  0.0 26.2 %shard_map.37 = (f32[4,256,2048]{2,1,0:T(8,128)S(1)}, f32[2,64,2176]{2,1,0:T(8,128)S(1)}, f32[64,2176]{1,0:T(8,128)S(1)}, f32[2,8,128]{2,1,0:T(8,128)S(1)}, f32[8,128]{1,0:T(8,128)S(1)}) custom-call(f32[4,256,2048]{2,1,0:T(8,128)} %values.1, s32[1,2048]{1,0:T(1,128)} %bitcast.2, s32[1,2048]{1,0:T(1,128)} %bitcast.3), custom_call_target="tpu_custom_call" | custom-call | tf_op jit(solution)/shard_map/pallas_call | solution.py:676
  26.2 3.3 %shard_map.38 = f32[4,256,2048]{2,1,0:T(8,128)} custom-call(f32[4,256,2048]{2,1,0:T(8,128)S(1)} %get-tuple-element.10.out, f32[2,64,2176]{2,1,0:T(8,128)S(1)} %get-tuple-element.11.rolled, f32[64,2176]{1,0:T(8,128)S(1)} %get-tuple-element.12.head_weight, f32[2,8,128]{2,1,0:T(8,128)S(1)} %get-tuple-element.13.advised, f32[8,128]{1,0:T(8,128)S(1)} %get-tuple-element.14.head_count), custom_call_target="tpu_custom_call" | custom-call | tf_op jit(solution)/shard_map/pallas_call | solution.py:708

commit v10 on v9

--- a/solution.py
+++ b/solution.py
@@ -385,7 +385,7 @@
             out[f, here, cols] = deviate * factor
 
     def roll_only(u, low, size):
-        @pl.loop(low, low + size, unroll=min(2, size))
+        @pl.loop(low, low + size, unroll=min(UNROLL, size))
         def chunk(c):
             cols = chunk_columns(c)
             rolled[u, :, cols] = window_means(own + u, 0, c)
@@ -622,7 +622,8 @@
         pltpu.make_async_copy(head.at[u], result.at[own + u, :WINDOW], sem)
         for u in range(helped)
     ]
-    for copy in copies + done[:own]:
+    whole = [pltpu.make_async_copy(out.at[f], result.at[f], sem) for f in range(own)]
+    for copy in whole + copies[own:]:
         copy.start()
 
     @pl.when(tm == 0)

time: 29.8 us -> 29.8 us (level)
  no operation moved by 1% of the time
where the time goes in v10:
time: 29.8 us; the launch traced here: 29.5 us
  Pallas kernels  29.5 us (99%)
    pallas_call x1, Pallas kernels, per_device(): pl.pallas_call(functools.partial(kernel, n_tm, n_as), out_shape=parts, in...  26.2 us
    pallas_call x1, Pallas kernels, per_device(): pl.pallas_call(functools.partial(finisher, own), out_shape=jax.ShapeDtype...  3.29 us

profile of v10, /device:TPU:1, one launch (start us, length us, event | category | flops | bytes accessed | tf_op | source)
XLA Modules:
  0.0 29.5 jit_solution(7265219361167250524)
XLA Ops:
  0.0 26.2 %shard_map.37 = (f32[4,256,2048]{2,1,0:T(8,128)S(1)}, f32[2,64,2176]{2,1,0:T(8,128)S(1)}, f32[64,2176]{1,0:T(8,128)S(1)}, f32[2,8,128]{2,1,0:T(8,128)S(1)}, f32[8,128]{1,0:T(8,128)S(1)}) custom-call(f32[4,256,2048]{2,1,0:T(8,128)} %values.1, s32[1,2048]{1,0:T(1,128)} %bitcast.2, s32[1,2048]{1,0:T(1,128)} %bitcast.3), custom_call_target="tpu_custom_call" | custom-call | tf_op jit(solution)/shard_map/pallas_call | solution.py:677
  26.2 3.3 %shard_map.38 = f32[4,256,2048]{2,1,0:T(8,128)} custom-call(f32[4,256,2048]{2,1,0:T(8,128)S(1)} %get-tuple-element.10.out, f32[2,64,2176]{2,1,0:T(8,128)S(1)} %get-tuple-element.11.rolled, f32[64,2176]{1,0:T(8,128)S(1)} %get-tuple-element.12.head_weight, f32[2,8,128]{2,1,0:T(8,128)S(1)} %get-tuple-element.13.advised, f32[8,128]{1,0:T(8,128)S(1)} %get-tuple-element.14.head_count), custom_call_target="tpu_custom_call" | custom-call | tf_op jit(solution)/shard_map/pallas_call | solution.py:709

commit v11 on v10

--- a/solution.py
+++ b/solution.py
@@ -639,7 +639,7 @@
             center, scale = columns_of[2 * u, :WINDOW, :], columns_of[2 * u, WINDOW:, :]
             middle, factor = columns_of[2 * u + 1, :WINDOW, :], columns_of[2 * u + 1, WINDOW:, :]
 
-            @pl.loop(0, assets // LANES, unroll=2)
+            @pl.loop(0, assets // LANES, unroll=UNROLL)
             def chunk(c):
                 cols = chunk_columns(c)
                 scored = (rolled[u, :, cols] - center) * scale

time: 29.8 us -> 29.8 us (level)
  no operation moved by 1% of the time
where the time goes in v11:
time: 29.8 us; the launch traced here: 29.5 us
  Pallas kernels  29.5 us (99%)
    pallas_call x1, Pallas kernels, per_device(): pl.pallas_call(functools.partial(kernel, n_tm, n_as), out_shape=parts, in...  26.2 us
    pallas_call x1, Pallas kernels, per_device(): pl.pallas_call(functools.partial(finisher, own), out_shape=jax.ShapeDtype...  3.29 us

profile of v11, /device:TPU:1, one launch (start us, length us, event | category | flops | bytes accessed | tf_op | source)
XLA Modules:
  0.0 29.5 jit_solution(15862555825944800332)
XLA Ops:
  0.0 26.2 %shard_map.37 = (f32[4,256,2048]{2,1,0:T(8,128)S(1)}, f32[2,64,2176]{2,1,0:T(8,128)S(1)}, f32[64,2176]{1,0:T(8,128)S(1)}, f32[2,8,128]{2,1,0:T(8,128)S(1)}, f32[8,128]{1,0:T(8,128)S(1)}) custom-call(f32[4,256,2048]{2,1,0:T(8,128)} %values.1, s32[1,2048]{1,0:T(1,128)} %bitcast.2, s32[1,2048]{1,0:T(1,128)} %bitcast.3), custom_call_target="tpu_custom_call" | custom-call | tf_op jit(solution)/shard_map/pallas_call | solution.py:677
  26.2 3.3 %shard_map.38 = f32[4,256,2048]{2,1,0:T(8,128)} custom-call(f32[4,256,2048]{2,1,0:T(8,128)S(1)} %get-tuple-element.10.out, f32[2,64,2176]{2,1,0:T(8,128)S(1)} %get-tuple-element.11.rolled, f32[64,2176]{1,0:T(8,128)S(1)} %get-tuple-element.12.head_weight, f32[2,8,128]{2,1,0:T(8,128)S(1)} %get-tuple-element.13.advised, f32[8,128]{1,0:T(8,128)S(1)} %get-tuple-element.14.head_count), custom_call_target="tpu_custom_call" | custom-call | tf_op jit(solution)/shard_map/pallas_call | solution.py:709
